TPU v7x, 256 devices: a whole 4x4x8 slice. The times are simulated.
256 devices in a mesh: rep: 1, dp: 256 (over x, y, z, core).
Axes of the slice: x: 4, y: 4, z: 8, core: 2. Of those that a mesh axis runs over, the one named last changes fastest.
Arguments:
- x: bfloat16 [256, 1024, 768], P(('rep', 'dp'))
- dy: bfloat16 [256, 1024, 768], P(('rep', 'dp'))
- w_gate: bfloat16 [2, 768, 2048], replicated
- w_up: bfloat16 [2, 768, 2048], replicated
- w_down: bfloat16 [2, 2048, 768], replicated
- m_w_gate: float32 [2, 768, 2048], replicated
- m_w_up: float32 [2, 768, 2048], replicated
- m_w_down: float32 [2, 2048, 768], replicated
- v_w_gate: float32 [2, 768, 2048], replicated
- v_w_up: float32 [2, 768, 2048], replicated
- v_w_down: float32 [2, 2048, 768], replicated
Outputs:
- output 1: bfloat16 [2, 768, 2048], P('rep')
- output 2: bfloat16 [2, 768, 2048], P('rep')
- output 3: bfloat16 [2, 2048, 768], P('rep')
- output 4: float32 [2, 768, 2048], P('rep')
- output 5: float32 [2, 768, 2048], P('rep')
- output 6: float32 [2, 2048, 768], P('rep')
- output 7: float32 [2, 768, 2048], P('rep')
- output 8: float32 [2, 768, 2048], P('rep')
- output 9: float32 [2, 2048, 768], P('rep')
All inputs are finite; a program needn't handle non-finite values.
Results may differ from a plain program's by a relative error of at most 0.022.
Values are sent between devices in bfloat16 or wider.
A program may use at most 768 MiB of HBM per device.

v0:
```python
import jax
import jax.numpy as jnp
from jax import lax
from jax.sharding import PartitionSpec as P

NAMES = ("w_gate", "w_up", "w_down")


def matmul(a, w):
    return jnp.dot(a, w, preferred_element_type=jnp.float32).astype(jnp.bfloat16)


def normed(h):
    wide = h.astype(jnp.float32)
    scale = lax.rsqrt(jnp.mean(wide**2, -1, keepdims=True) + 1e-6)
    return (wide * scale).astype(jnp.bfloat16)


def layer(h, w):
    a = normed(h)
    gate = jnp.dot(a, w["w_gate"], preferred_element_type=jnp.float32)
    up = jnp.dot(a, w["w_up"], preferred_element_type=jnp.float32)
    return h + matmul((jax.nn.silu(gate) * up).astype(jnp.bfloat16), w["w_down"])


def adamw(w, m, v, g):
    m = 0.9 * m + 0.1 * g
    v = 0.95 * v + 0.05 * g * g
    step = m * lax.rsqrt(v + 1e-8) + 0.1 * w
    return (w - 0.02 * step).astype(jnp.bfloat16), m, v


def solution(mesh):
    def step(x, dy, *arrays):
        weights, m, v = (arrays[i : i + 3] for i in (0, 3, 6))
        layers = weights[0].shape[0]
        h, kept = x[0], []
        for number in range(layers):
            kept.append(h)
            h = layer(h, {name: w[number] for name, w in zip(NAMES, weights, strict=True)})
        by_h, summed = dy[0], [None] * layers
        for number in reversed(range(layers)):
            _, back = jax.vjp(lambda w, h: layer(h, w), {name: w[number] for name, w in zip(NAMES, weights, strict=True)}, kept[number])
            by_w, by_h = back(by_h)
            summed[number] = [lax.psum(by_w[name], "dp") for name in NAMES]
        gradients = [jnp.stack([summed[number][i] for number in range(layers)]).astype(jnp.float32) for i in range(3)]
        new = [adamw(w.astype(jnp.float32), m, v, g) for w, m, v, g in zip(weights, m, v, gradients, strict=True)]
        return tuple(one[which] for which in range(3) for one in new)

    return jax.shard_map(
        step,
        mesh=mesh,
        in_specs=(P(("rep", "dp"), None, None),) * 2 + (P(None, None, None),) * 9,
        out_specs=(P("rep", None, None),) * 9,
        check_vma=False,
    )
```

profile of v0, /device:TPU:2, one launch (start us, length us, event | category | flops | bytes accessed | tf_op | source)
XLA Modules:
  0.0 505.0 jit_solution(7237714320206994310)
XLA Ops:
  7.2 0.0 all-reduce.3.cloned.1.call-start
  7.2 1.7 copy.20
  8.9 0.0 copy-start
  9.0 0.4 fusion.36
  9.3 0.8 copy-done
  10.1 0.0 slice-start
  10.1 2.7 copy.21
  12.8 0.0 slice-start.1
  12.8 0.0 copy-start.3
  12.8 8.0 %convolution_convert_fusion.1 = bf16[1024,2048]{1,0:T(8,128)(2,1)} fusion(bf16[2,2048,768]{2,1,0:T(8,128)(2,1)} %param.15, bf16[1,1024,768]{2,1,0:T(8,128)(2,1)} %param.12), kind=kOutput, calls=%fused_computation.62 | convolution fusion | flops 3223322624 | bytes 8912896 | tf_op jit(solution)/shard_map/transpose(jvp())/dot_general | solution.py:10
  20.8 0.0 slice-done
  20.8 0.0 slice-done.1
  20.8 0.0 copy-done.3
  20.8 0.0 slice-start.6
  20.9 0.0 slice-start.4
  20.9 5.7 %fusion.56 = f32[1024,2048]{1,0:T(8,128)} fusion(bf16[2,768,2048]{2,1,0:T(8,128)(2,1)S(1)} %bitcast.81, bf16[1,1024,768]{2,1,0:T(8,128)(2,1)S(1)} %copy-done.3, f32[1024]{0:T(1024)S(1)} %add_rsqrt_fusion), kind=kOutput, calls=%fused_computation.89 | convolution fusion | flops 3223584768 | bytes 13111296 | tf_op jit(solution)/shard_map/dot_general | solution.py:21
  26.6 0.0 slice-start.7
  26.6 10.0 %multiply_convert_fusion.1 = (bf16[1024,2048]{1,0:T(8,128)(2,1)}, f32[1024,2048]{1,0:T(8,128)}) fusion(f32[1024,2048]{1,0:T(8,128)} %fusion.56, bf16[2,768,2048]{2,1,0:T(8,128)(2,1)} %param.14, bf16[1,1024,768]{2,1,0:T(8,128)(2,1)S(1)} %copy-done.3, f32[1024]{0:T(1024)S(1)} %add_rsqrt_fusion), kind=kOutput, calls=%fused_computation.44 | convolution fusion | flops 3236167680 | bytes 25694208 | tf_op jit(solution)/shard_map/dot_general | solution.py:22
  36.6 0.0 slice-done.6
  36.6 0.0 slice-done.7
  36.6 0.0 copy-done.1
  36.7 6.0 %fusion.40 = (f32[1024]{0:T(1024)S(1)}, bf16[1024,768]{0,1:T(8,128)(2,1)S(1)}) fusion(bf16[1024,2048]{1,0:T(8,128)(2,1)} %get-tuple-element.24, bf16[2,2048,768]{2,1,0:T(8,128)(2,1)S(1)} %bitcast.87, bf16[1,1024,768]{1,2,0:T(8,128)(2,1)S(1)} %copy-done.1), kind=kOutput, calls=%fused_computation.73 | convolution fusion | flops 3225156608 | bytes 10489856 | tf_op jit(solution)/shard_map/dot_general | solution.py:10
  42.7 0.0 copy-start.5
  42.7 0.0 slice-done.4
  42.7 0.0 slice-done.5
  42.7 5.7 %fusion.43 = f32[1024,2048]{1,0:T(8,128)} fusion(bf16[2,768,2048]{2,1,0:T(8,128)(2,1)S(1)} %bitcast.85, bf16[1024,768]{0,1:T(8,128)(2,1)S(1)} %get-tuple-element.27, f32[1024]{0:T(1024)S(1)} %fusion.102), kind=kOutput, calls=%fused_computation.76 | convolution fusion | flops 3223584768 | bytes 13111296 | tf_op jit(solution)/shard_map/jvp()/dot_general | solution.py:22
  48.5 0.0 copy-done.5
  48.5 12.3 %fusion.17 = (bf16[1024,2048]{1,0:T(8,128)(2,1)}, f32[1024,2048]{1,0:T(8,128)}) fusion(f32[1024,2048]{1,0:T(8,128)} %fusion.43, bf16[1024,2048]{1,0:T(8,128)(2,1)} %convolution_convert_fusion.1, bf16[2,768,2048]{2,1,0:T(8,128)(2,1)S(1)} %bitcast.81, bf16[1024,768]{0,1:T(8,128)(2,1)S(1)} %get-tuple-element.27, f32[1024]{0:T(1024)S(1)} %fusion.102), kind=kOutput, calls=%fused_computation.35 | convolution fusion | flops 3248750592 | bytes 29888512 | tf_op jit(solution)/shard_map/jvp()/dot_general | solution.py:21
  60.7 9.5 %fusion.81 = bf16[1024,768]{0,1:T(8,128)(2,1)} fusion(bf16[2,768,2048]{2,1,0:T(8,128)(2,1)S(1)} %bitcast.85, bf16[1024,2048]{1,0:T(8,128)(2,1)} %convolution_convert_fusion.1, f32[1024,2048]{1,0:T(8,128)} %get-tuple-element.29), kind=kOutput, calls=%fused_computation.109 | convolution fusion | flops 3234594816 | bytes 17301504 | tf_op jit(solution)/shard_map/transpose(jvp())/dot_general | solution.py:22
  70.2 0.0 copy-done.6
  70.2 10.0 %fusion.67 = bf16[1,768,2048]{2,1,0:T(8,128)(2,1)} fusion(bf16[1024,2048]{1,0:T(8,128)(2,1)} %convolution_convert_fusion.1, bf16[1024,768]{0,1:T(8,128)(2,1)S(1)} %copy-done.6, f32[1024]{0:T(1024)S(1)} %fusion.102, f32[1024,2048]{1,0:T(8,128)} %get-tuple-element.29), kind=kOutput, calls=%fused_computation.99 | convolution fusion | flops 3237740544 | bytes 17305600 | tf_op jit(solution)/shard_map/transpose(jvp())/dot_general | solution.py:22
  80.2 0.0 copy-done.4
  80.2 12.1 %fusion.68 = bf16[1,2048,768]{2,1,0:T(8,128)(2,1)} fusion(f32[1024,2048]{1,0:T(8,128)} %fusion.43, bf16[1,1024,768]{2,1,0:T(8,128)(2,1)S(1)} %copy-done.4, f32[1024,2048]{1,0:T(8,128)} %get-tuple-element.29), kind=kOutput, calls=%fused_computation.100 | convolution fusion | flops 3235381248 | bytes 21495808 | tf_op jit(solution)/shard_map/transpose(jvp())/dot_general | solution.py:10
  92.4 0.0 copy-done.7
  92.4 0.0 copy-done.9
  92.4 0.0 copy-start.12
  92.4 5.0 fusion.64
  97.4 0.0 copy-done.10
  97.4 0.0 copy-done.12
  97.4 3.7 fusion.42
  101.1 0.0 copy-done.2
  101.1 1.1 fusion.85
  102.2 0.0 copy-start.11
  102.2 0.0 slice-start.8
  102.2 3.7 convolution_convert_fusion
  106.0 0.0 copy-done.11
  106.0 0.0 copy-start.8
  106.0 0.0 slice-start.9
  106.0 0.0 slice-start.10
  106.0 5.0 fusion.65
  111.0 0.0 copy-done.8
  111.0 0.0 slice-done.8
  111.0 0.0 slice-done.9
  111.0 0.0 slice-start.11
  111.0 5.1 %fusion.66 = bf16[1,768,2048]{2,1,0:T(8,128)(2,1)} fusion(bf16[1024,2048]{1,0:T(8,128)(2,1)S(1)} %convolution_convert_fusion, f32[1024,2048]{1,0:T(8,128)S(1)} %bitcast.89, bf16[1,1024,768]{1,2,0:T(8,128)(2,1)S(1)} %copy-done.1, f32[1024]{0:T(1024)S(1)} %add_rsqrt_fusion), kind=kOutput, calls=%fused_computation.98 | convolution fusion | flops 3237740544 | bytes 17305600 | tf_op jit(solution)/shard_map/transpose(jvp())/dot_general | solution.py:22
  116.2 0.0 slice-done.10
  116.2 0.0 slice-done.11
  116.2 7.9 %fusion.61 = bf16[1,768,2048]{2,1,0:T(8,128)(2,1)} fusion(f32[1024,2048]{1,0:T(8,128)S(1)} %bitcast.89, f32[1024,2048]{1,0:T(8,128)S(1)} %bitcast.91, bf16[1024,2048]{1,0:T(8,128)(2,1)} %copy-done.8, bf16[1,1024,768]{1,2,0:T(8,128)(2,1)S(1)} %copy-done.1, f32[1024]{0:T(1024)S(1)} %add_rsqrt_fusion), kind=kOutput, calls=%fused_computation.95 | convolution fusion | flops 3248226304 | bytes 25694208 | tf_op jit(solution)/shard_map/transpose(jvp())/dot_general | solution.py:21
  124.0 0.0 all-reduce.3.cloned.1.call-update
  124.1 307.4 %all-reduce.3.cloned.1.call-done = (bf16[1,768,2048]{2,1,0:T(8,128)(2,1)}, bf16[1,768,2048]{2,1,0:T(8,128)(2,1)}, bf16[1,768,2048]{2,1,0:T(8,128)(2,1)}, bf16[1,...) async-done(((bf16[1,768,2048]{2,1,0:T(8,128)(2,1)}, bf16[1,768,2048]{2,1,0:T(8,128)(2,1)}, bf16[1,768,2048]{2,1,0:T(8,128)(2,1)}, ...) | async-done | bytes 18874384 | tf_op jit(solution)/shard_map/psum | solution.py:45
  431.5 24.5 %fusion.10 = (bf16[2,2048,768]{2,1,0:T(8,128)(2,1)}, f32[2,2048,768]{2,1,0:T(8,128)}, f32[2,2048,768]{2,1,0:T(8,128)}) fusion(bf16[2,2048,768]{2,1,0:T(8,128)(2,1)} %param.15, bf16[1,2048,768]{2,1,0:T(8,128)(2,1)} %get-tuple-element.13, bf16[1,2048,768]{2,1,0:T(8,128)(2,1)} %get-tuple-element.14, f32[2,2048,768]{2,1,0:T(8,128)} %param.21, ...), kind=kLoop, calls=%fused_computation.22 | loop fusion | flops 59768832 | bytes 69206016 | tf_op jit(solution)/shard_map/convert_element_type | solution.py:30
  456.1 0.0 slice-done.2
  456.1 0.0 slice-done.3
  456.1 41.8 %fusion.2 = (bf16[2,768,2048]{2,1,0:T(8,128)(2,1)}, f32[2,768,2048]{2,1,0:T(8,128)}, f32[2,768,2048]{2,1,0:T(8,128)}, bf16[2,768,2048]{2,1,0:T(8,128)(2,1)}, f32...) fusion(bf16[2,768,2048]{2,1,0:T(8,128)(2,1)S(1)} %bitcast.83, bf16[1,768,2048]{2,1,0:T(8,128)(2,1)} %get-tuple-element.9, ...), kind=kLoop, calls=%fused_computation.14 | loop fusion | flops 119537664 | bytes 138412032 | tf_op jit(solution)/shard_map/convert_element_type | solution.py:30
  (19 shorter events, 0.0 us)
Async XLA Ops:
  7.2 424.3 %all-reduce.3.cloned.1.call-start = ((), (), s32[]{:S(2)}) async-start(), calls=%async_computation | async-start | bytes 37748736 | tf_op jit(solution)/shard_map/psum | solution.py:45
  8.9 1.1 copy-start
  10.1 10.7 %slice-start = ((s8[6291456]{0:T(1024)(128)(4,1)}), s8[2097152]{0:T(1024)(128)(4,1)S(1)}, s32[]{:S(2)}) async-start(s8[6291456]{0:T(1024)(128)(4,1)} %bitcast.80), calls=%async_computation.1 | async-start | bytes 4194304
  12.8 8.0 %slice-start.1 = ((s8[6291456]{0:T(1024)(128)(4,1)}), s8[4194304]{0:T(1024)(128)(4,1)S(1)}, s32[]{:S(2)}) async-start(s8[6291456]{0:T(1024)(128)(4,1)} %bitcast.80), calls=%async_computation.2 | async-start | bytes 8388608
  12.8 8.0 %copy-start.3 = (bf16[1,1024,768]{2,1,0:T(8,128)(2,1)S(1)}, bf16[1,1024,768]{2,1,0:T(8,128)(2,1)}, u32[]{:S(2)}) copy-start(bf16[1,1024,768]{2,1,0:T(8,128)(2,1)} %param.11) | copy-start | bytes 4718596
  20.8 15.8 %slice-start.6 = ((s8[6291456]{0:T(1024)(128)(4,1)}), s8[4194304]{0:T(1024)(128)(4,1)S(1)}, s32[]{:S(2)}) async-start(s8[6291456]{0:T(1024)(128)(4,1)} %bitcast.86), calls=%async_computation.7 | async-start | bytes 8388608
  20.9 21.8 %slice-start.4 = ((s8[6291456]{0:T(1024)(128)(4,1)}), s8[4194304]{0:T(1024)(128)(4,1)S(1)}, s32[]{:S(2)}) async-start(s8[6291456]{0:T(1024)(128)(4,1)} %bitcast.84), calls=%async_computation.5 | async-start | bytes 8388608
  26.6 10.1 %slice-start.7 = ((s8[6291456]{0:T(1024)(128)(4,1)}), s8[2097152]{0:T(1024)(128)(4,1)S(1)}, s32[]{:S(2)}) async-start(s8[6291456]{0:T(1024)(128)(4,1)} %bitcast.86), calls=%async_computation.8 | async-start | bytes 4194304
  26.6 10.1 %copy-start.1 = (bf16[1,1024,768]{1,2,0:T(8,128)(2,1)S(1)}, bf16[1,1024,768]{1,2,0:T(8,128)(2,1)}, u32[]{:S(2)}) copy-start(bf16[1,1024,768]{1,2,0:T(8,128)(2,1)} %copy-done) | copy-start | bytes 4718596
  26.6 16.1 %slice-start.5 = ((s8[6291456]{0:T(1024)(128)(4,1)}), s8[2097152]{0:T(1024)(128)(4,1)S(1)}, s32[]{:S(2)}) async-start(s8[6291456]{0:T(1024)(128)(4,1)} %bitcast.84), calls=%async_computation.6 | async-start | bytes 4194304
  42.7 5.8 %copy-start.5 = (bf16[1024,768]{0,1:T(8,128)(2,1)}, bf16[1024,768]{0,1:T(8,128)(2,1)S(1)}, u32[]{:S(2)}) copy-start(bf16[1024,768]{0,1:T(8,128)(2,1)S(1)} %get-tuple-element.27) | copy-start | bytes 4718596
  60.7 9.5 %copy-start.6 = (bf16[1024,768]{0,1:T(8,128)(2,1)S(1)}, bf16[1024,768]{0,1:T(8,128)(2,1)}, u32[]{:S(2)}) copy-start(bf16[1024,768]{0,1:T(8,128)(2,1)} %copy-done.5) | copy-start | bytes 4718596
  70.2 10.0 %copy-start.4 = (bf16[1,1024,768]{2,1,0:T(8,128)(2,1)S(1)}, bf16[1,1024,768]{2,1,0:T(8,128)(2,1)}, u32[]{:S(2)}) copy-start(bf16[1,1024,768]{2,1,0:T(8,128)(2,1)} %param.12) | copy-start | bytes 4718596
  80.2 12.1 %copy-start.7 = (bf16[1024,768]{0,1:T(8,128)(2,1)S(1)}, bf16[1024,768]{0,1:T(8,128)(2,1)}, u32[]{:S(2)}) copy-start(bf16[1024,768]{0,1:T(8,128)(2,1)} %copy-done.5) | copy-start | bytes 4718596
  80.2 12.1 %copy-start.9 = (bf16[1024,2048]{1,0:T(8,128)(2,1)S(1)}, bf16[1024,2048]{1,0:T(8,128)(2,1)}, u32[]{:S(2)}) copy-start(bf16[1024,2048]{1,0:T(8,128)(2,1)} %get-tuple-element.28) | copy-start | bytes 12582916
  92.4 5.0 copy-start.10
  92.4 5.0 copy-start.12
  97.4 3.7 copy-start.2
  102.2 3.8 copy-start.11
  102.2 8.8 %slice-start.8 = ((s8[8388608]{0:T(1024)(128)(4,1)}), s8[4194304]{0:T(1024)(128)(4,1)S(1)}, s32[]{:S(2)}) async-start(s8[8388608]{0:T(1024)(128)(4,1)} %bitcast.88), calls=%async_computation.9 | async-start | bytes 8388608
  106.0 5.0 copy-start.8
  106.0 5.0 slice-start.9
  106.0 10.2 %slice-start.10 = ((s8[8388608]{0:T(1024)(128)(4,1)}), s8[4194304]{0:T(1024)(128)(4,1)S(1)}, s32[]{:S(2)}) async-start(s8[8388608]{0:T(1024)(128)(4,1)} %bitcast.90), calls=%async_computation.11 | async-start | bytes 8388608
  111.0 5.1 %slice-start.11 = ((s8[8388608]{0:T(1024)(128)(4,1)}), s8[4194304]{0:T(1024)(128)(4,1)S(1)}, s32[]{:S(2)}) async-start(s8[8388608]{0:T(1024)(128)(4,1)} %bitcast.90), calls=%async_computation.12 | async-start | bytes 8388608
  124.0 332.0 %slice-start.2 = ((s8[6291456]{0:T(1024)(128)(4,1)}), s8[2097152]{0:T(1024)(128)(4,1)S(1)}, s32[]{:S(2)}) async-start(s8[6291456]{0:T(1024)(128)(4,1)} %bitcast.82), calls=%async_computation.3 | async-start | bytes 4194304
  431.5 24.6 %slice-start.3 = ((s8[6291456]{0:T(1024)(128)(4,1)}), s8[4194304]{0:T(1024)(128)(4,1)S(1)}, s32[]{:S(2)}) async-start(s8[6291456]{0:T(1024)(128)(4,1)} %bitcast.82), calls=%async_computation.4 | async-start | bytes 8388608
Sparse Core Ops, SparseCore 0:
  124.2 307.2 all-reduce.2
where the time goes:
time: 514 us; the launch traced here: 505 us
  waiting for transfers between devices  307 us (60%)
  matrix products  110 us (21%)
  other arithmetic  67.9 us (13%)
  between operations  14.5 us (3%)
  local copies, waits for them, and re-layouts  5.35 us (1%)
    psum x1, waiting for transfers between devices, step(): summed[number] = [lax.psum(by_w[name], 'dp') for name in NAMES]  307 us
    convert_element_type x2, other arithmetic, adamw(): return ((w - 0.02 * step).astype(jnp.bfloat16), m, v)  66.4 us
    dot_general x5, matrix products, layer(): up = jnp.dot(a, w['w_up'], preferred_element_type=jnp.float32)  40.4 us
    dot_general x5, matrix products, matmul(): jnp.dot(a, w, preferred_element_type=jnp.float32).astype(jnp.bfloat16)  34.8 us
    dot_general x5, matrix products, layer(): gate = jnp.dot(a, w['w_gate'], preferred_element_type=jnp.float32)  34.5 us
  transfers between devices with their start and end apart: 1, of which 1 were waited for; matrix products, arithmetic and copies ran while one was open for 0% of the time, Pallas kernels for 0%

commit v1 on v0

v1 whole, which is shorter than its diff:
```python
import functools

import jax
import jax.numpy as jnp
from jax import lax
from jax.experimental import pallas as pl
from jax.experimental.pallas import tpu as pltpu
from jax.sharding import PartitionSpec as P

NAMES = ("w_gate", "w_up", "w_down")
MESH = pl.DeviceIdType.MESH
F32, BF16 = jnp.float32, jnp.bfloat16
DIMS = (4, 4, 8)
ORDERS = ((0, 1, 2), (1, 2, 0), (2, 0, 1))
UNITS = 128
SHAPES = ((768, 2048), (768, 2048), (2048, 768))


def matmul(a, w):
    return jnp.dot(a, w, preferred_element_type=jnp.float32).astype(jnp.bfloat16)


def normed(h):
    wide = h.astype(jnp.float32)
    scale = lax.rsqrt(jnp.mean(wide**2, -1, keepdims=True) + 1e-6)
    return (wide * scale).astype(jnp.bfloat16)


def layer(h, w):
    a = normed(h)
    gate = jnp.dot(a, w["w_gate"], preferred_element_type=jnp.float32)
    up = jnp.dot(a, w["w_up"], preferred_element_type=jnp.float32)
    return h + matmul((jax.nn.silu(gate) * up).astype(jnp.bfloat16), w["w_down"])


def piece_scratch(kind):
    a, b, c = (DIMS[d] for d in ORDERS[kind])
    rows, cols = SHAPES[kind]
    u1, u2, u3 = UNITS // a, UNITS // a // b, UNITS // a // b // c
    dma = pltpu.SemaphoreType.DMA
    out = {
        "own": pltpu.VMEM((rows // 2, cols), BF16),
        "rec": pltpu.VMEM((rows // 2, cols), BF16),
        "acc1": pltpu.VMEM((u1, 48, 128), F32),
        "acc2": pltpu.VMEM((u2, 48, 128), F32),
        "core": dma((3,)),
    }
    if a > 1:
        out |= {
            "rs": pltpu.VMEM((2, a - 1, u1 // 2, 48, 128), BF16),
            "rr": pltpu.VMEM((2, a - 1, u1 // 2, 48, 128), BF16),
            "r_sem": dma((2, 2, a - 1)),
        }
    if b > 1:
        out |= {"bs": pltpu.VMEM((b - 1, u2, 48, 128), BF16), "br": pltpu.VMEM((b - 1, u2, 48, 128), BF16), "b_sem": dma((2, b - 1))}
    if c > 1:
        out |= {"cs": pltpu.VMEM((c - 1, u3, 48, 128), BF16), "cr": pltpu.VMEM((c - 1, u3, 48, 128), BF16), "c_sem": dma((2, c - 1))}
    return out


class Place:
    def __init__(self):
        self.me = lax.axis_index("dp")
        nx, ny, nz = DIMS
        self.core = lax.rem(self.me, 2)
        self.at = (self.me // (2 * ny * nz), lax.rem(self.me // (2 * nz), ny), lax.rem(self.me // 2, nz))
        self.stride = (2 * ny * nz, 2 * nz, 2)

    def peer(self, dim, away):
        n = DIMS[dim]
        return self.me + (lax.rem(self.at[dim] + away, n) - self.at[dim]) * self.stride[dim]

    def partner(self):
        return self.me + 1 - 2 * self.core


def remote(src, dst, send, recv, device):
    return pltpu.make_async_remote_copy(
        src_ref=src, dst_ref=dst, send_sem=send, recv_sem=recv, device_id={"dp": device}, device_id_type=MESH
    )


def gather_half(kind, s, unit, count, arrived, dst, base):
    own, rec = s["own"], s["rec"]
    if kind < 2:
        row0 = (unit // 16) * 48

        def body(q, _):
            row = pl.multiple_of(row0 + q * 16, 16)
            block, sub = q // 3, pl.multiple_of(lax.rem(q, 3) * 16, 16)
            for col in range(16):
                lanes = slice(col * 128, (col + 1) * 128)
                x = own[pl.ds(row, 16), lanes].astype(F32) + rec[pl.ds(row, 16), lanes].astype(F32)
                if arrived is not None:
                    x = x + arrived[block * 16 + col, pl.ds(sub, 16), :].astype(F32)
                dst[base + block * 16 + col, pl.ds(sub, 16), :] = x.astype(dst.dtype)
            return 0

        lax.fori_loop(0, count // 16 * 3, body, 0)
    else:
        row0 = (unit // 2) * 16

        def body(q, _):
            row = pl.multiple_of(row0 + q * 16, 16)
            for col in range(6):
                lanes, at, sub = slice(col * 128, (col + 1) * 128), 2 * q + col // 3, slice(col % 3 * 16, col % 3 * 16 + 16)
                x = own[pl.ds(row, 16), lanes].astype(F32) + rec[pl.ds(row, 16), lanes].astype(F32)
                if arrived is not None:
                    x = x + arrived[at, sub, :].astype(F32)
                dst[base + at, sub, :] = x.astype(dst.dtype)
            return 0

        lax.fori_loop(0, count // 2, body, 0)


def piece_stages(kind, g, out, s, here, started):
    da, db, dc = ORDERS[kind]
    a, b, c = DIMS[da], DIMS[db], DIMS[dc]
    u1, u2, u3 = UNITS // a, UNITS // a // b, UNITS // a // b // c
    half, rows = u1 // 2, SHAPES[kind][0] // 2
    state = {}

    def begin():
        other = pl.multiple_of((1 - here.core) * rows, 16)
        mine = pl.multiple_of(here.core * rows, 16)
        state["core"] = remote(g.at[pl.ds(other, rows)], s["rec"], s["core"].at[0], s["core"].at[1], here.partner())
        state["core"].start()
        started.append(state["core"])
        state["own"] = pltpu.make_async_copy(g.at[pl.ds(mine, rows)], s["own"], s["core"].at[2])
        state["own"].start()

    def ring_copy(way, step):
        to = here.peer(da, 1 if way == 0 else a - 1)
        return remote(s["rs"].at[way, step], s["rr"].at[way, step], s["r_sem"].at[0, way, step], s["r_sem"].at[1, way, step], to)

    def chunk(way, step):
        i = here.at[da]
        j = lax.rem(i + 2 * a - 1 - step, a) if way == 0 else lax.rem(i + 1 + step, a)
        return j * u1 + way * half

    def ring_send(way, step, arrived):
        gather_half(kind, s, chunk(way, step), half, arrived, s["rs"].at[way, step], 0)
        copy = ring_copy(way, step)
        copy.start()
        started.append(copy)
        state[way, step] = copy

    def first():
        state["own"].wait()
        state["core"].wait_recv()
        if a == 1:
            gather_half(kind, s, 0, u1, None, s["acc1"], 0)
            b_send()
        for way in range(2 if a > 1 else 0):
            ring_send(way, 0, None)

    def ring_step(step):
        for way in range(2):
            state[way, step].wait_recv()
            arrived = s["rr"].at[way, step]
            if step < a - 2:
                ring_send(way, step + 1, arrived)
            else:
                gather_half(kind, s, chunk(way, a - 1), half, arrived, s["acc1"], way * half)
        if step == a - 2:
            b_send()

    def direct_send(n, dim, units, acc, send, recv, sem, name):
        for d in range(1, n):
            j = lax.rem(here.at[dim] + d, n)

            def body(k, _, j=j, d=d):
                send[d - 1, k] = acc[j * units + k].astype(BF16)
                return 0

            lax.fori_loop(0, units, body, 0)
            copy = remote(send.at[d - 1], recv.at[d - 1], sem.at[0, d - 1], sem.at[1, d - 1], here.peer(dim, d))
            copy.start()
            started.append(copy)
            state[name, d] = copy

    def b_send():
        if b > 1:
            direct_send(b, db, u2, s["acc1"], s["bs"], s["br"], s["b_sem"], "b")

    def b_recv():
        for d in range(1, b):
            state["b", d].wait_recv()

        def body(k, _):
            x = s["acc1"][here.at[db] * u2 + k]
            for d in range(1, b):
                x = x + s["br"][d - 1, k].astype(F32)
            s["acc2"][k] = x
            return 0

        lax.fori_loop(0, u2, body, 0)
        if c > 1:
            direct_send(c, dc, u3, s["acc2"], s["cs"], s["cr"], s["c_sem"], "c")

    def c_recv():
        for d in range(1, c):
            state["c", d].wait_recv()

        def body(k, _):
            x = s["acc2"][here.at[dc] * u3 + k]
            for d in range(1, c):
                x = x + s["cr"][d - 1, k].astype(F32)
            out[k] = x.astype(BF16)
            return 0

        lax.fori_loop(0, u3, body, 0)

    stages = [begin, first] + [functools.partial(ring_step, step) for step in range(a - 1)] + [b_recv, c_recv]
    ring_us = 8.5 if a == 4 else 4.6
    return stages, ring_us


def scatter_kernel(kinds, names, *refs):
    pieces = len(kinds)
    grads, outs, scratch = refs[:pieces], refs[pieces : 2 * pieces], refs[2 * pieces :]
    here = Place()
    barrier = pltpu.get_barrier_semaphore()
    peers = [here.partner()] + [here.peer(dim, away) for dim in range(3) for away in range(1, DIMS[dim])]
    for peer in peers:
        pl.semaphore_signal(barrier, inc=1, device_id={"dp": peer}, device_id_type=MESH)
    pl.semaphore_wait(barrier, len(peers))

    order, started = [], []
    for n, kind in enumerate(kinds):
        s, scratch = dict(zip(names[n], scratch)), scratch[len(names[n]) :]
        stages, ring_us = piece_stages(kind, grads[n], outs[n], s, here, started)
        when = 3.0 + 2.6 * n
        for k, stage in enumerate(stages):
            order.append((0.1 * n - 100 if k == 0 else when, len(order), stage))
            if k >= 1:
                when += ring_us if k < len(stages) - 2 else 7.0
    for _, _, stage in sorted(order, key=lambda entry: entry[:2]):
        stage()
    for copy in started:
        copy.wait_send()


def reduce_scatter(grads, kinds):
    specs = [piece_scratch(kind) for kind in kinds]
    units = UNITS // (DIMS[0] * DIMS[1] * DIMS[2])
    return pl.pallas_call(
        functools.partial(scatter_kernel, kinds, [tuple(spec) for spec in specs]),
        out_shape=[jax.ShapeDtypeStruct((units, 48, 128), BF16)] * len(kinds),
        in_specs=[pl.BlockSpec(memory_space=pl.ANY)] * len(kinds),
        out_specs=[pl.BlockSpec(memory_space=pltpu.VMEM)] * len(kinds),
        scratch_shapes=[shape for spec in specs for shape in spec.values()],
        compiler_params=pltpu.CompilerParams(collective_id=0, has_side_effects=True, vmem_limit_bytes=60 * 2**20),
        cost_estimate=pl.CostEstimate(flops=50_000_000, bytes_accessed=30_000_000, transcendentals=0),
        name="reduce_scatter",
    )(*grads)


def adamw(w, m, v, g):
    m = 0.9 * m + 0.1 * g
    v = 0.95 * v + 0.05 * g * g
    step = m * lax.rsqrt(v + 1e-8) + 0.1 * w
    return (w - 0.02 * step).astype(BF16), m, v


def adamw_kernel(kind, g_ref, w_ref, m_ref, v_ref, *rest):
    new_w, new_m, new_v = rest[-3:]

    def tile(g, rows, lanes):
        at = (0, rows, lanes)
        new_w[at], new_m[at], new_v[at] = adamw(w_ref[at].astype(F32), m_ref[at], v_ref[at], g.astype(F32))

    order = ORDERS[kind]
    span = {0: (1, 2, 8), 1: (4, 1, 4), 2: (4, 4, 1)}[kind]
    units = []
    sizes = [span[d] for d in order]
    for i in range(sizes[0]):
        for j in range(sizes[1]):
            for k in range(sizes[2]):
                at = [0, 0, 0]
                at[order[0]], at[order[1]], at[order[2]] = i, j, k
                units.append(tuple(at))
    for n, (x, y, z) in enumerate(units):
        if kind < 2:
            tile(g_ref[x, y, z, 0], slice(None), slice(n * 128, (n + 1) * 128))
        else:
            for k in range(3):
                lane = (n % 2 * 3 + k) * 128
                tile(g_ref[x, y, z, 0, 16 * k : 16 * k + 16], slice(n // 2 * 16, n // 2 * 16 + 16), slice(lane, lane + 128))


def adamw_call(kind, number, g, w, m, v, before):
    rows, cols = SHAPES[kind]
    block = pl.BlockSpec((1, rows // 16, cols), lambda i: (number, i, 0))
    if kind == 0:
        g_spec = pl.BlockSpec((1, 2, 8, 1, 48, 128), lambda i: (i % 8 // 2, i % 2, 0, i // 8, 0, 0))
    elif kind == 1:
        g_spec = pl.BlockSpec((4, 1, 4, 1, 48, 128), lambda i: (0, i % 8 // 2, i % 2, i // 8, 0, 0))
    else:
        g_spec = pl.BlockSpec((4, 4, 1, 1, 48, 128), lambda i: (0, 0, i % 8, i // 8, 0, 0))
    before = before or ()
    return pl.pallas_call(
        functools.partial(adamw_kernel, kind),
        grid=(16,),
        out_shape=[jax.ShapeDtypeStruct(x.shape, x.dtype) for x in (w, m, v)],
        in_specs=[g_spec, block, block, block] + [pl.BlockSpec(memory_space=pl.ANY)] * len(before),
        out_specs=[block] * 3,
        input_output_aliases={4 + i: i for i in range(len(before))},
        compiler_params=pltpu.CompilerParams(dimension_semantics=("arbitrary",), vmem_limit_bytes=60 * 2**20),
        cost_estimate=pl.CostEstimate(flops=rows * cols * 200, bytes_accessed=rows * cols * 22, transcendentals=rows * cols),
        name=f"adamw_{NAMES[kind]}",
    )(g, w, m, v, *before)


def solution(mesh):
    def step(x, dy, *arrays):
        weights, m, v = (arrays[i : i + 3] for i in (0, 3, 6))
        layers = weights[0].shape[0]
        h, kept = x[0], []
        for number in range(layers):
            kept.append(h)
            h = layer(h, {name: w[number] for name, w in zip(NAMES, weights, strict=True)})
        by_h, grads = dy[0], {}
        for number in reversed(range(layers)):
            _, back = jax.vjp(lambda w, h: layer(h, w), {name: w[number] for name, w in zip(NAMES, weights, strict=True)}, kept[number])
            by_w, by_h = back(by_h)
            for kind, name in enumerate(NAMES):
                grads[number, kind] = by_w[name]
        keys = [(number, kind) for number in reversed(range(layers)) for kind in range(3)]
        shards = reduce_scatter([grads[key] for key in keys], [kind for _, kind in keys])
        new = [None] * 3
        for (number, kind), shard in zip(keys, shards):
            g = lax.all_gather(shard[0], "dp").reshape(*DIMS, 2, 48, 128)
            new[kind] = adamw_call(kind, number, g, weights[kind], m[kind], v[kind], new[kind])
        return tuple(one[which] for which in range(3) for one in new)

    return jax.shard_map(
        step,
        mesh=mesh,
        in_specs=(P(("rep", "dp"), None, None),) * 2 + (P(None, None, None),) * 9,
        out_specs=(P("rep", None, None),) * 9,
        check_vma=False,
    )
```

time: 514 us -> 892 us (1.74)
  waiting for transfers between devices: 307 us -> 551 us
  Pallas kernels: 0 us -> 194 us
  other arithmetic: 67.9 us -> 1.52 us
    all_gather x0 -> x6, waiting for transfers between devices: none -> 548 us  [step(): g = lax.all_gather(shard[0], 'dp').reshape(*DIMS, 2, 48, 128)]
    psum x1 -> x0, waiting for transfers between devices: 307 us -> none  [step(): summed[number] = [lax.psum(by_w[name], 'dp') for name in NAMES]]
    pallas_call x0 -> x7, Pallas kernels: none -> 194 us  [the longest x6 107 us: adamw_call(): pl.pallas_call(functools.partial(adamw_kernel, kind), grid=(16,), out_sha...]
    convert_element_type x2 -> x0, other arithmetic: 66.4 us -> none  [adamw(): return ((w - 0.02 * step).astype(jnp.bfloat16), m, v)]
  transfers between devices with their start and end apart: 1 -> 6, of which waited for: 1 -> 6; matrix products, arithmetic and copies ran while one was open for 0% -> 0% of each run, Pallas kernels for 0% -> 10%
where the time goes in v1:
time: 892 us; the launch traced here: 879 us
  waiting for transfers between devices  551 us (62%)
  Pallas kernels  194 us (22%)
  matrix products  111 us (12%)
  between operations  14.5 us (2%)
    all_gather x6, waiting for transfers between devices, step(): g = lax.all_gather(shard[0], 'dp').reshape(*DIMS, 2, 48, 128)  548 us
    pallas_call x6, Pallas kernels, adamw_call(): pl.pallas_call(functools.partial(adamw_kernel, kind), grid=(16,), out_sha...  107 us
    pallas_call x1, Pallas kernels, reduce_scatter(): pl.pallas_call(functools.partial(scatter_kernel, kinds, [tuple(spec) for...  86.7 us
    dot_general x5, matrix products, layer(): up = jnp.dot(a, w['w_up'], preferred_element_type=jnp.float32)  38.3 us
    dot_general x5, matrix products, layer(): gate = jnp.dot(a, w['w_gate'], preferred_element_type=jnp.float32)  37.9 us
    dot_general x5, matrix products, matmul(): jnp.dot(a, w, preferred_element_type=jnp.float32).astype(jnp.bfloat16)  34.6 us
  transfers between devices with their start and end apart: 6, of which 6 were waited for; matrix products, arithmetic and copies ran while one was open for 0% of the time, Pallas kernels for 10%

profile of v1, /device:TPU:2, one launch (start us, length us, event | category | flops | bytes accessed | tf_op | source)
XLA Modules:
  0.0 879.0 jit_solution(7116727594942027942)
XLA Ops:
  7.2 0.0 all-gather.17.cloned.1.call-start
  7.2 1.7 copy.31
  8.9 0.0 copy-start
  9.0 0.4 fusion.21
  9.3 0.8 copy-done
  10.1 2.7 copy.32
  12.8 8.0 convolution_convert_fusion.1
  20.8 0.0 copy-done.3
  20.8 7.9 fusion.41
  28.7 0.0 slice-done.2
  28.7 0.0 slice-done.3
  28.7 0.0 copy-start.1
  28.8 0.0 slice-start.5
  28.8 9.1 %multiply_convert_fusion.1 = (bf16[1024,2048]{1,0:T(8,128)(2,1)}, f32[1024,2048]{1,0:T(8,128)}) fusion(f32[1024,2048]{1,0:T(8,128)} %fusion.41, bf16[2,768,2048]{2,1,0:T(8,128)(2,1)S(1)} %bitcast.77, bf16[1,1024,768]{2,1,0:T(8,128)(2,1)S(1)} %copy-done.3, f32[1024]{0:T(1024)S(1)} %add_rsqrt_fusion), kind=kOutput, calls=%fused_computation.17 | convolution fusion | flops 3236167680 | bytes 25694208 | tf_op jit(solution)/shard_map/dot_general | solution.py:32
  37.9 0.0 slice-done
  37.9 0.0 slice-done.1
  37.9 0.0 copy-done.1
  37.9 6.0 fusion.25
  43.9 0.0 copy-start.5
  43.9 1.1 copy-done.5
  45.1 5.7 fusion.33
  50.8 0.0 slice-done.4
  50.8 0.0 slice-done.5
  50.8 12.9 %fusion.2 = (bf16[1024,2048]{1,0:T(8,128)(2,1)}, f32[1024,2048]{1,0:T(8,128)}) fusion(f32[1024,2048]{1,0:T(8,128)} %fusion.33, bf16[1024,2048]{1,0:T(8,128)(2,1)} %convolution_convert_fusion.1, bf16[2,768,2048]{2,1,0:T(8,128)(2,1)S(1)} %bitcast.79, bf16[1024,768]{0,1:T(8,128)(2,1)} %copy-done.5, f32[1024]{0:T(1024)S(1)} %fusion.79), kind=kOutput, calls=%fused_computation.8 | convolution fusion | flops 3248750592 | bytes 29888512 | tf_op jit(solution)/shard_map/jvp()/dot_general | solution.py:31
  63.7 0.0 copy-done.4
  63.7 12.0 %fusion.15.refs_2_ = bf16[2048,768]{1,0:T(8,128)(2,1)} fusion(f32[1024,2048]{1,0:T(8,128)} %fusion.33, bf16[1,1024,768]{2,1,0:T(8,128)(2,1)S(1)} %copy-done.4, f32[1024,2048]{1,0:T(8,128)} %get-tuple-element.62), kind=kOutput, calls=%fused_computation.33 | convolution fusion | flops 3235381248 | bytes 21495808 | tf_op jit(solution)/shard_map/transpose(jvp())/dot_general | solution.py:20
  75.6 8.3 fusion.58
  83.9 0.0 copy-start.7
  83.9 10.0 %fusion.19.refs_1_ = bf16[768,2048]{1,0:T(8,128)(2,1)} fusion(bf16[1024,2048]{1,0:T(8,128)(2,1)} %convolution_convert_fusion.1, bf16[1024,768]{0,1:T(8,128)(2,1)S(1)} %copy-done.6, f32[1024]{0:T(1024)S(1)} %fusion.79, f32[1024,2048]{1,0:T(8,128)} %get-tuple-element.62), kind=kOutput, calls=%fused_computation.35 | convolution fusion | flops 3237740544 | bytes 17305600 | tf_op jit(solution)/shard_map/transpose(jvp())/dot_general | solution.py:32
  94.0 0.0 copy-done.7
  94.0 5.0 convolution_convert_fusion.3.refs_0_
  99.0 3.7 fusion.27
  102.6 0.0 copy-start.8
  102.7 0.0 slice-start.6
  102.7 1.1 fusion.62
  103.8 1.0 copy-done.8
  104.8 4.9 convolution_convert_fusion.2.refs_5_
  109.8 3.7 convolution_convert_fusion
  113.5 5.1 fusion.20.refs_4_
  118.6 8.5 fusion.16.refs_3_
  127.1 86.7 %reduce_scatter.1 = (bf16[1,48,128]{2,1,0:T(8,128)(2,1)}, bf16[1,48,128]{2,1,0:T(8,128)(2,1)}, bf16[1,48,128]{2,1,0:T(8,128)(2,1)}, bf16[1,48,128]{2,1,0:T(8,128...) custom-call(bf16[768,2048]{1,0:T(8,128)(2,1)} %convolution_convert_fusion.3.refs_0_, ...), custom_call_target="tpu_custom_call" | custom-call | flops 50000000 | bytes 30000000 | tf_op jit(solution)/shard_map/reduce_scatter/pallas_call | solution.py:247
  213.8 0.0 all-gather.17.cloned.1.call-update
  213.8 0.0 all-gather.13.cloned.1.call-start
  213.9 0.7 all-gather.13.cloned.1.call-update
  214.6 0.0 all-gather.9.cloned.1.call-start
  214.6 0.7 all-gather.9.cloned.1.call-update
  215.3 0.0 all-gather.15.cloned.1.call-start
  215.3 0.5 all-gather.15.cloned.1.call-update
  215.9 0.0 all-gather.11.cloned.1.call-start
  215.9 0.5 all-gather.11.cloned.1.call-update
  216.5 0.0 all-gather.7.cloned.1.call-start
  216.5 0.5 all-gather.7.cloned.1.call-update
  217.0 98.9 %all-gather.17.cloned.1.call-done = bf16[256,48,128]{2,1,0:T(8,128)(2,1)} async-done(((bf16[1,48,128]{2,1,0:T(8,128)(2,1)}), bf16[256,48,128]{2,1,0:T(8,128)(2,1)}) %all-gather.17.cloned.1.call-update) | async-done | bytes 3145744 | tf_op jit(solution)/shard_map/all_gather | solution.py:333
  315.9 17.9 %adamw_w_down.2 = (bf16[2,2048,768]{2,1,0:T(8,128)(2,1)}, f32[2,2048,768]{2,1,0:T(8,128)}, f32[2,2048,768]{2,1,0:T(8,128)}) custom-call(bf16[4,4,8,2,48,128]{5,4,3,2,1,0:T(8,128)(2,1)} %bitcast.83, bf16[2,2048,768]{2,1,0:T(8,128)(2,1)} %w_ref.11, f32[2,2048,768]{2,1,0:T(8,128)} %m_ref.11, f32[2,2048,768]{2,1,0:T(8,128)} %v_ref.11), custom_call_target="tpu_custom_call" | custom-call | flops 314572800 | bytes 34603008 | tf_op jit(solution)/shard_map/adamw_w_down/pallas_call | solution.py:302
  333.7 89.9 %all-gather.13.cloned.1.call-done = bf16[256,48,128]{2,1,0:T(8,128)(2,1)} async-done(((bf16[1,48,128]{2,1,0:T(8,128)(2,1)}), bf16[256,48,128]{2,1,0:T(8,128)(2,1)}) %all-gather.13.cloned.1.call-update) | async-done | bytes 3145744 | tf_op jit(solution)/shard_map/all_gather | solution.py:333
  423.6 17.9 %adamw_w_up.2 = (bf16[2,768,2048]{2,1,0:T(8,128)(2,1)}, f32[2,768,2048]{2,1,0:T(8,128)}, f32[2,768,2048]{2,1,0:T(8,128)}) custom-call(bf16[4,4,8,2,48,128]{5,4,3,2,1,0:T(8,128)(2,1)} %bitcast.84, bf16[2,768,2048]{2,1,0:T(8,128)(2,1)} %w_ref.9, f32[2,768,2048]{2,1,0:T(8,128)} %m_ref.9, f32[2,768,2048]{2,1,0:T(8,128)} %v_ref.9), custom_call_target="tpu_custom_call" | custom-call | flops 314572800 | bytes 34603008 | tf_op jit(solution)/shard_map/adamw_w_up/pallas_call | solution.py:302
  441.5 89.9 %all-gather.9.cloned.1.call-done = bf16[256,48,128]{2,1,0:T(8,128)(2,1)} async-done(((bf16[1,48,128]{2,1,0:T(8,128)(2,1)}), bf16[256,48,128]{2,1,0:T(8,128)(2,1)}) %all-gather.9.cloned.1.call-update) | async-done | bytes 3145744 | tf_op jit(solution)/shard_map/all_gather | solution.py:333
  531.4 17.8 %adamw_w_gate.2 = (bf16[2,768,2048]{2,1,0:T(8,128)(2,1)}, f32[2,768,2048]{2,1,0:T(8,128)}, f32[2,768,2048]{2,1,0:T(8,128)}) custom-call(bf16[4,4,8,2,48,128]{5,4,3,2,1,0:T(8,128)(2,1)} %bitcast.85, bf16[2,768,2048]{2,1,0:T(8,128)(2,1)} %w_ref.7, f32[2,768,2048]{2,1,0:T(8,128)} %m_ref.7, f32[2,768,2048]{2,1,0:T(8,128)} %v_ref.7), custom_call_target="tpu_custom_call" | custom-call | flops 314572800 | bytes 34603008 | tf_op jit(solution)/shard_map/adamw_w_gate/pallas_call | solution.py:302
  549.2 89.8 %all-gather.15.cloned.1.call-done = bf16[256,48,128]{2,1,0:T(8,128)(2,1)} async-done(((bf16[1,48,128]{2,1,0:T(8,128)(2,1)}), bf16[256,48,128]{2,1,0:T(8,128)(2,1)}) %all-gather.15.cloned.1.call-update) | async-done | bytes 3145744 | tf_op jit(solution)/shard_map/all_gather | solution.py:333
  638.9 17.9 %adamw_w_down.3 = (bf16[2,2048,768]{2,1,0:T(8,128)(2,1)}, f32[2,2048,768]{2,1,0:T(8,128)}, f32[2,2048,768]{2,1,0:T(8,128)}) custom-call(bf16[4,4,8,2,48,128]{5,4,3,2,1,0:T(8,128)(2,1)} %bitcast.82, bf16[2,2048,768]{2,1,0:T(8,128)(2,1)} %w_ref.11, f32[2,2048,768]{2,1,0:T(8,128)} %m_ref.11, ...), custom_call_target="tpu_custom_call", output_to_operand_aliasing={{0}: (4, {}), {1}: (5, {}), {2}: (6, {})} | custom-call | flops 314572800 | bytes 34603008 | tf_op jit(solution)/shard_map/adamw_w_down/pallas_call | solution.py:302
  656.8 89.7 %all-gather.11.cloned.1.call-done = bf16[256,48,128]{2,1,0:T(8,128)(2,1)} async-done(((bf16[1,48,128]{2,1,0:T(8,128)(2,1)}), bf16[256,48,128]{2,1,0:T(8,128)(2,1)}) %all-gather.11.cloned.1.call-update) | async-done | bytes 3145744 | tf_op jit(solution)/shard_map/all_gather | solution.py:333
  746.5 17.9 %adamw_w_up.3 = (bf16[2,768,2048]{2,1,0:T(8,128)(2,1)}, f32[2,768,2048]{2,1,0:T(8,128)}, f32[2,768,2048]{2,1,0:T(8,128)}) custom-call(bf16[4,4,8,2,48,128]{5,4,3,2,1,0:T(8,128)(2,1)} %bitcast.81, bf16[2,768,2048]{2,1,0:T(8,128)(2,1)} %w_ref.9, f32[2,768,2048]{2,1,0:T(8,128)} %m_ref.9, ...), custom_call_target="tpu_custom_call", output_to_operand_aliasing={{0}: (4, {}), {1}: (5, {}), {2}: (6, {})} | custom-call | flops 314572800 | bytes 34603008 | tf_op jit(solution)/shard_map/adamw_w_up/pallas_call | solution.py:302
  764.4 89.7 %all-gather.7.cloned.1.call-done = bf16[256,48,128]{2,1,0:T(8,128)(2,1)} async-done(((bf16[1,48,128]{2,1,0:T(8,128)(2,1)}), bf16[256,48,128]{2,1,0:T(8,128)(2,1)}) %all-gather.7.cloned.1.call-update) | async-done | bytes 3145744 | tf_op jit(solution)/shard_map/all_gather | solution.py:333
  854.1 17.8 %adamw_w_gate.3 = (bf16[2,768,2048]{2,1,0:T(8,128)(2,1)}, f32[2,768,2048]{2,1,0:T(8,128)}, f32[2,768,2048]{2,1,0:T(8,128)}) custom-call(bf16[4,4,8,2,48,128]{5,4,3,2,1,0:T(8,128)(2,1)} %bitcast.80, bf16[2,768,2048]{2,1,0:T(8,128)(2,1)} %w_ref.7, f32[2,768,2048]{2,1,0:T(8,128)} %m_ref.7, ...), custom_call_target="tpu_custom_call", output_to_operand_aliasing={{0}: (4, {}), {1}: (5, {}), {2}: (6, {})} | custom-call | flops 314572800 | bytes 34603008 | tf_op jit(solution)/shard_map/adamw_w_gate/pallas_call | solution.py:302
  (21 shorter events, 0.0 us)
Async XLA Ops:
  7.2 308.7 %all-gather.17.cloned.1.call-start = ((), (), s32[]{:S(2)}) async-start(), calls=%async_computation.5 | async-start | bytes 3158016 | tf_op jit(solution)/shard_map/all_gather | solution.py:333
  8.9 1.1 copy-start
  10.1 18.6 %slice-start.2 = ((s8[6291456]{0:T(1024)(128)(4,1)}), s8[2097152]{0:T(1024)(128)(4,1)S(1)}, s32[]{:S(2)}) async-start(s8[6291456]{0:T(1024)(128)(4,1)} %bitcast.76), calls=%async_computation.8 | async-start | bytes 4194304
  12.8 8.0 copy-start.3
  12.8 15.9 %slice-start.3 = ((s8[6291456]{0:T(1024)(128)(4,1)}), s8[4194304]{0:T(1024)(128)(4,1)S(1)}, s32[]{:S(2)}) async-start(s8[6291456]{0:T(1024)(128)(4,1)} %bitcast.76), calls=%async_computation.9 | async-start | bytes 8388608
  20.8 17.1 %slice-start = ((s8[6291456]{0:T(1024)(128)(4,1)}), s8[4194304]{0:T(1024)(128)(4,1)S(1)}, s32[]{:S(2)}) async-start(s8[6291456]{0:T(1024)(128)(4,1)} %bitcast.74), calls=%async_computation.6 | async-start | bytes 8388608
  20.8 30.0 %slice-start.4 = ((s8[6291456]{0:T(1024)(128)(4,1)}), s8[4194304]{0:T(1024)(128)(4,1)S(1)}, s32[]{:S(2)}) async-start(s8[6291456]{0:T(1024)(128)(4,1)} %bitcast.78), calls=%async_computation.10 | async-start | bytes 8388608
  28.7 9.2 %slice-start.1 = ((s8[6291456]{0:T(1024)(128)(4,1)}), s8[2097152]{0:T(1024)(128)(4,1)S(1)}, s32[]{:S(2)}) async-start(s8[6291456]{0:T(1024)(128)(4,1)} %bitcast.74), calls=%async_computation.7 | async-start | bytes 4194304
  28.7 9.2 %copy-start.1 = (bf16[1,1024,768]{1,2,0:T(8,128)(2,1)S(1)}, bf16[1,1024,768]{1,2,0:T(8,128)(2,1)}, u32[]{:S(2)}) copy-start(bf16[1,1024,768]{1,2,0:T(8,128)(2,1)} %copy-done) | copy-start | bytes 4718596
  28.8 22.0 %slice-start.5 = ((s8[6291456]{0:T(1024)(128)(4,1)}), s8[2097152]{0:T(1024)(128)(4,1)S(1)}, s32[]{:S(2)}) async-start(s8[6291456]{0:T(1024)(128)(4,1)} %bitcast.78), calls=%async_computation.11 | async-start | bytes 4194304
  43.9 1.1 copy-start.5
  50.8 12.9 %copy-start.4 = (bf16[1,1024,768]{2,1,0:T(8,128)(2,1)S(1)}, bf16[1,1024,768]{2,1,0:T(8,128)(2,1)}, u32[]{:S(2)}) copy-start(bf16[1,1024,768]{2,1,0:T(8,128)(2,1)} %param.12) | copy-start | bytes 4718596
  75.6 8.3 copy-start.6
  83.9 10.0 %copy-start.7 = (bf16[1024,2048]{1,0:T(8,128)(2,1)S(1)}, bf16[1024,2048]{1,0:T(8,128)(2,1)}, u32[]{:S(2)}) copy-start(bf16[1024,2048]{1,0:T(8,128)(2,1)} %get-tuple-element.61) | copy-start | bytes 12582916
  99.0 3.7 copy-start.2
  102.6 2.2 copy-start.8
  102.7 10.8 %slice-start.6 = ((s8[8388608]{0:T(1024)(128)(4,1)}), s8[4194304]{0:T(1024)(128)(4,1)S(1)}, s32[]{:S(2)}) async-start(s8[8388608]{0:T(1024)(128)(4,1)} %bitcast.86), calls=%async_computation.12 | async-start | bytes 8388608
  104.8 8.7 slice-start.7
  213.8 209.8 %all-gather.13.cloned.1.call-start = ((), (), s32[]{:S(2)}) async-start(), calls=%async_computation.3 | async-start | bytes 3158016 | tf_op jit(solution)/shard_map/all_gather | solution.py:333
  214.6 316.8 %all-gather.9.cloned.1.call-start = ((), (), s32[]{:S(2)}) async-start(), calls=%async_computation.1 | async-start | bytes 3158016 | tf_op jit(solution)/shard_map/all_gather | solution.py:333
  215.3 423.7 %all-gather.15.cloned.1.call-start = ((), (), s32[]{:S(2)}) async-start(), calls=%async_computation.4 | async-start | bytes 3158016 | tf_op jit(solution)/shard_map/all_gather | solution.py:333
  215.9 530.7 %all-gather.11.cloned.1.call-start = ((), (), s32[]{:S(2)}) async-start(), calls=%async_computation.2 | async-start | bytes 3158016 | tf_op jit(solution)/shard_map/all_gather | solution.py:333
  216.5 637.7 %all-gather.7.cloned.1.call-start = ((), (), s32[]{:S(2)}) async-start(), calls=%async_computation | async-start | bytes 3158016 | tf_op jit(solution)/shard_map/all_gather | solution.py:333
Sparse Core Ops, SparseCore 0:
  213.9 101.9 all-gather.16
  319.4 104.1 all-gather.12
  427.2 104.1 all-gather.8
  534.8 104.1 all-gather.14
  642.3 104.1 all-gather.10
  749.9 104.1 all-gather.6

commit v2 on v0

--- a/solution.py
+++ b/solution.py
@@ -1,9 +1,20 @@
+import functools
+
 import jax
 import jax.numpy as jnp
 from jax import lax
+from jax.experimental import pallas as pl
+from jax.experimental.pallas import tpu as pltpu
 from jax.sharding import PartitionSpec as P
 
 NAMES = ("w_gate", "w_up", "w_down")
+MESH = pl.DeviceIdType.MESH
+F32, BF16 = jnp.float32, jnp.bfloat16
+DIMS = (4, 4, 8)
+UNITS = 128
+SHAPES = ((768, 2048), (768, 2048), (2048, 768))
+ORDERS = (("x", "y", "z"), ("y", "x", "z"), ("z", "x", "y"), ("xy", "yx", "z"))
+MINE = ((1, 0, 3), (0, 2, 2), (0, 1, 1), (0, 0, 0))
 
 
 def matmul(a, w):
@@ -21,6 +32,320 @@
     gate = jnp.dot(a, w["w_gate"], preferred_element_type=jnp.float32)
     up = jnp.dot(a, w["w_up"], preferred_element_type=jnp.float32)
     return h + matmul((jax.nn.silu(gate) * up).astype(jnp.bfloat16), w["w_down"])
+
+
+class Axis:
+    def __init__(self, me, n, at, stride):
+        self.me, self.n, self.at, self.stride = me, n, at, stride
+
+    def peer(self, away):
+        return self.me + (lax.rem(self.at + away, self.n) - self.at) * self.stride
+
+
+class Place:
+    def __init__(self):
+        me = lax.axis_index("dp")
+        nx, ny, nz = DIMS
+        self.me, self.core = me, lax.rem(me, 2)
+        x, y, z = me // (2 * ny * nz), lax.rem(me // (2 * nz), ny), lax.rem(me // 2, nz)
+        sx, sy, core = 2 * ny * nz, 2 * nz, self.core
+        self.axes = {"x": Axis(me, nx, x, sx), "y": Axis(me, ny, y, sy), "z": Axis(me, nz, z, 2)}
+        self.axes["xy"] = Axis(me, nx, x + core * (y - x), sx + core * (sy - sx)) if nx == ny else self.axes["x"]
+        self.axes["yx"] = Axis(me, ny, y + core * (x - y), sy + core * (sx - sy)) if nx == ny else self.axes["y"]
+        self.partner = me + 1 - 2 * core
+
+
+def sizes(order):
+    nx, ny, nz = DIMS
+    n = {"x": nx, "y": ny, "z": nz, "xy": nx, "yx": ny}
+    return tuple(n[axis] for axis in ORDERS[order])
+
+
+def piece_scratch(kind, order):
+    a, b, c = sizes(order)
+    rows, cols = SHAPES[kind]
+    u1, u2, u3 = UNITS // a, UNITS // a // b, UNITS // a // b // c
+    dma = pltpu.SemaphoreType.DMA
+    out = {
+        "own": pltpu.VMEM((rows // 2, cols), BF16),
+        "rec": pltpu.VMEM((rows // 2, cols), BF16),
+        "all": pltpu.VMEM((UNITS, 48, 128), BF16),
+        "acc1": pltpu.VMEM((u1, 48, 128), F32),
+        "acc2": pltpu.VMEM((u2, 48, 128), F32),
+        "core": dma((3,)),
+        "end": dma((3, 1 + 2 * max(a // 2, 1))),
+    }
+    for name, n, units in (("a", a, u1), ("b", b, u2)):
+        if n > 1:
+            out[name + "s"] = pltpu.VMEM((2, n // 2, units, 48, 128), BF16)
+            out[name + "r"] = pltpu.VMEM((2, n // 2, units, 48, 128), BF16)
+            out[name + "_sum"] = dma((2, 2, n // 2))
+            out[name + "_all"] = dma((2, 2, n // 2))
+    if c > 1:
+        out |= {"cs": pltpu.VMEM((c - 1, u3, 48, 128), BF16), "cr": pltpu.VMEM((c - 1, u3, 48, 128), BF16)}
+        out |= {"c_sum": dma((2, c - 1)), "c_all": dma((2, c - 1))}
+    return out
+
+
+def remote(src, dst, send, recv, device):
+    return pltpu.make_async_remote_copy(
+        src_ref=src, dst_ref=dst, send_sem=send, recv_sem=recv, device_id={"dp": device}, device_id_type=MESH
+    )
+
+
+def first_row(kind, unit):
+    return pl.multiple_of((unit // 16) * 48 if kind < 2 else (unit // 2) * 16, 16)
+
+
+def row_count(kind, count):
+    return count // 16 * 48 if kind < 2 else count // 2 * 16
+
+
+def tiles(kind, unit, count, tile):
+    row0 = first_row(kind, unit)
+
+    def body(q, _):
+        rows = pl.ds(pl.multiple_of(row0 + q * 16, 16), 16)
+        for col in range(16 if kind < 2 else 6):
+            lanes = slice(col * 128, (col + 1) * 128)
+            if kind < 2:
+                tile(rows, lanes, q // 3 * 16 + col, pl.ds(pl.multiple_of(lax.rem(q, 3) * 16, 16), 16))
+            else:
+                tile(rows, lanes, 2 * q + col // 3, slice(col % 3 * 16, col % 3 * 16 + 16))
+        return 0
+
+    lax.fori_loop(0, row_count(kind, count) // 16, body, 0)
+
+
+def piece_stages(kind, order, g, out, s, here, started):
+    axes = [here.axes[name] for name in ORDERS[order]]
+    a, b, c = sizes(order)
+    u1, u2, u3 = UNITS // a, UNITS // a // b, UNITS // a // b // c
+    rows = SHAPES[kind][0] // 2
+    ia, ib, ic = (axis.at for axis in axes)
+    base_b = ia * u1
+    base_c = base_b + ib * u2
+    base = base_c + ic * u3
+    state = {}
+
+    def go(key, copy):
+        copy.start()
+        started.append(copy.wait_send)
+        state[key] = copy
+
+    def begin():
+        other = pl.multiple_of((1 - here.core) * rows, 16)
+        mine = pl.multiple_of(here.core * rows, 16)
+        go("core", remote(g.at[pl.ds(other, rows)], s["rec"], s["core"].at[0], s["core"].at[1], here.partner))
+        state["own"] = pltpu.make_async_copy(g.at[pl.ds(mine, rows)], s["own"], s["core"].at[2])
+        state["own"].start()
+
+    def add_a(unit, count, arrived, dst, at):
+        def tile(rows, lanes, n, sub):
+            x = s["own"][rows, lanes].astype(F32) + s["rec"][rows, lanes].astype(F32)
+            for ref, skip in arrived:
+                x = x + ref[skip + n, sub, :].astype(F32)
+            dst[at + n, sub, :] = x.astype(dst.dtype)
+
+        tiles(kind, unit, count, tile)
+
+    def add_b(unit, count, arrived, dst, at):
+        def body(n, _):
+            x = s["acc1"][unit + n]
+            for ref, skip in arrived:
+                x = x + ref[skip + n].astype(F32)
+            dst[at + n] = x.astype(dst.dtype)
+            return 0
+
+        lax.fori_loop(0, count, body, 0)
+
+    def chain(name, axis, units, add, acc):
+        n, steps, half = axis.n, axis.n // 2, units // 2
+
+        def send(way, t):
+            far = steps - t
+            j = lax.rem(axis.at + (far if way == 0 else n - far), n)
+            buf = s[name + "s"].at[way, t]
+            got = s[name + "r"].at[way, t - 1] if t > 0 else None
+            long, short = way * half, (1 - way) * half
+            add(j * units + long, half, [(got, long)] if t > 0 else [], buf, long)
+            if t > 0:
+                add(j * units + short, half, [(got, short)] if t > 1 else [], buf, short)
+                src, dst = buf, s[name + "r"].at[way, t]
+            else:
+                src, dst = buf.at[pl.ds(long, half)], s[name + "r"].at[way, t, pl.ds(long, half)]
+            sem = s[name + "_sum"]
+            go((name, way, t), remote(src, dst, sem.at[0, way, t], sem.at[1, way, t], axis.peer(1 if way == 0 else n - 1)))
+
+        def start():
+            if n == 1:
+                add(0, units, [], acc, 0)
+                return
+            for way in range(2):
+                send(way, 0)
+
+        def step(t):
+            for way in range(2):
+                state[name, way, t].wait_recv()
+                if t + 1 < steps:
+                    send(way, t + 1)
+            if t + 1 == steps:
+                up, down = s[name + "r"].at[0, t], s[name + "r"].at[1, t]
+                j = axis.at * units
+                add(j, half, [(up, 0)] + ([(down, 0)] if t > 0 else []), acc, 0)
+                add(j + half, half, [(down, half)] + ([(up, half)] if t > 0 else []), acc, half)
+
+        return start, step
+
+    def c_start():
+        for d in range(1, c):
+            j = lax.rem(ic + d, c)
+            for k in range(u3):
+                s["cs"][d - 1, k] = s["acc2"][j * u3 + k].astype(BF16)
+            sem = s["c_sum"]
+            go(("c", d), remote(s["cs"].at[d - 1], s["cr"].at[d - 1], sem.at[0, d - 1], sem.at[1, d - 1], axes[2].peer(d)))
+
+    def c_step():
+        for d in range(1, c):
+            state["c", d].wait_recv()
+        for k in range(u3):
+            x = s["acc2"][ic * u3 + k]
+            for d in range(1, c):
+                x = x + s["cr"][d - 1, k].astype(F32)
+            s["all"][base + k] = x.astype(BF16)
+
+    def c_all_start():
+        mine = s["all"].at[pl.ds(base, u3)]
+        for d in range(1, c):
+            sem = s["c_all"]
+            go(("c_all", d), remote(mine, mine, sem.at[0, d - 1], sem.at[1, d - 1], axes[2].peer(d)))
+
+    def c_all_step():
+        for d in range(1, c):
+            state["c_all", d].wait_recv()
+
+    def spread(name, axis, units, first):
+        n, steps, half = axis.n, axis.n // 2, units // 2
+
+        def part(way, t, chunk):
+            whole = t + 1 < steps
+            return first + chunk * units + (0 if whole else way * half), units if whole else half
+
+        def send(way, t):
+            unit, count = part(way, t, lax.rem(axis.at + (n - t if way == 0 else t), n))
+            ref, sem = s["all"].at[pl.ds(unit, count)], s[name + "_all"]
+            go((name + "_all", way, t), remote(ref, ref, sem.at[0, way, t], sem.at[1, way, t], axis.peer(1 if way == 0 else n - 1)))
+
+        def start():
+            for way in range(2 if n > 1 else 0):
+                send(way, 0)
+
+        def step(t, then=None):
+            for way in range(2):
+                state[name + "_all", way, t].wait_recv()
+                if t + 1 < steps:
+                    send(way, t + 1)
+            for way in range(2 if then else 0):
+                unit, count = part(way, t, lax.rem(axis.at + (n - 1 - t if way == 0 else 1 + t), n))
+                then(unit, count, 1 + way * steps + t)
+
+        return start, step
+
+    def finish(unit, count, slot):
+        def tile(rows, lanes, n, sub):
+            s["own"][rows, lanes] = s["all"][unit + n, sub, :]
+
+        tiles(kind, unit, count, tile)
+        row, many = first_row(kind, unit), row_count(kind, count)
+        src = s["own"].at[pl.ds(row, many)]
+        dst = out.at[pl.ds(pl.multiple_of(here.core * rows + row, 16), many)]
+        copy = remote(src, dst, s["end"].at[0, slot], s["end"].at[1, slot], here.partner)
+        local = pltpu.make_async_copy(src, dst, s["end"].at[2, slot])
+        copy.start()
+        local.start()
+        started.extend([copy.wait_send, copy.wait_recv, local.wait])
+
+    a_start, a_step = chain("a", axes[0], u1, add_a, s["acc1"])
+    b_start, b_step = chain("b", axes[1], u2, add_b, s["acc2"])
+    b_all_start, b_all_step = spread("b", axes[1], u2, base_b)
+    a_all_start, a_all_step = spread("a", axes[0], u1, 0)
+
+    def join(*parts):
+        def run():
+            for part in parts:
+                part()
+
+        return run
+
+    def wait_core():
+        state["own"].wait()
+        state["core"].wait_recv()
+
+    def own_rows():
+        finish(base_b, u1, 0)
+
+    stages = [[wait_core, a_start]]
+    times = [2.0]
+    for t in range(a // 2):
+        stages.append([functools.partial(a_step, t)])
+        times.append({4: (7.0, 13.0)[t % 2], 8: 6.5}.get(a, 5.0))
+    stages[-1].append(b_start)
+    for t in range(b // 2):
+        stages.append([functools.partial(b_step, t)])
+        times.append(4.0)
+    stages[-1].append(c_start)
+    stages.append([c_step, c_all_start])
+    times.append(4.5)
+    stages.append([c_all_step, b_all_start])
+    times.append(4.5)
+    for t in range(b // 2):
+        stages.append([functools.partial(b_all_step, t)])
+        times.append(4.0)
+    stages[-1] += [a_all_start, own_rows]
+    for t in range(a // 2):
+        stages.append([functools.partial(a_all_step, t, finish)])
+        times.append({4: (13.0, 7.0)[t % 2], 8: 6.5}.get(a, 5.0))
+    return begin, [(join(*stage), time) for stage, time in zip(stages, times)]
+
+
+def sum_kernel(pieces, names, *refs):
+    count = len(pieces)
+    grads, outs, scratch = refs[:count], refs[count : 2 * count], refs[2 * count :]
+    here = Place()
+    barrier = pltpu.get_barrier_semaphore()
+    axes = [here.axes[name] for name in "xyz"]
+    peers = [here.partner] + [axis.peer(away) for axis in axes for away in range(1, axis.n)]
+    for peer in peers:
+        pl.semaphore_signal(barrier, inc=1, device_id={"dp": peer}, device_id_type=MESH)
+    pl.semaphore_wait(barrier, len(peers))
+
+    plan, started = [], []
+    for n, (kind, order) in enumerate(pieces):
+        s, scratch = dict(zip(names[n], scratch)), scratch[len(names[n]) :]
+        begin, stages = piece_stages(kind, order, grads[n], outs[n], s, here, started)
+        begin()
+        when = 2.4 * n
+        for stage, time in stages:
+            when += time
+            plan.append((when, len(plan), stage))
+    for _, _, stage in sorted(plan, key=lambda entry: entry[:2]):
+        stage()
+    for wait in started:
+        wait()
+
+
+def group_sum(grads, pieces):
+    specs = [piece_scratch(*piece) for piece in pieces]
+    return pl.pallas_call(
+        functools.partial(sum_kernel, pieces, [tuple(spec) for spec in specs]),
+        out_shape=[jax.ShapeDtypeStruct(g.shape, BF16) for g in grads],
+        in_specs=[pl.BlockSpec(memory_space=pl.ANY)] * len(pieces),
+        out_specs=[pl.BlockSpec(memory_space=pl.ANY)] * len(pieces),
+        scratch_shapes=[shape for spec in specs for shape in spec.values()],
+        compiler_params=pltpu.CompilerParams(collective_id=0, has_side_effects=True, vmem_limit_bytes=60 * 2**20),
+        cost_estimate=pl.CostEstimate(flops=300_000_000, bytes_accessed=60_000_000, transcendentals=0),
+        name="group_sum",
+    )(*grads)
 
 
 def adamw(w, m, v, g):
@@ -38,13 +363,17 @@
         for number in range(layers):
             kept.append(h)
             h = layer(h, {name: w[number] for name, w in zip(NAMES, weights, strict=True)})
-        by_h, summed = dy[0], [None] * layers
+        by_h, grads = dy[0], {}
         for number in reversed(range(layers)):
             _, back = jax.vjp(lambda w, h: layer(h, w), {name: w[number] for name, w in zip(NAMES, weights, strict=True)}, kept[number])
             by_w, by_h = back(by_h)
-            summed[number] = [lax.psum(by_w[name], "dp") for name in NAMES]
-        gradients = [jnp.stack([summed[number][i] for number in range(layers)]).astype(jnp.float32) for i in range(3)]
-        new = [adamw(w.astype(jnp.float32), m, v, g) for w, m, v, g in zip(weights, m, v, gradients, strict=True)]
+            for kind, name in enumerate(NAMES):
+                grads[number, kind] = by_w[name]
+        sums = {key: lax.psum(g, "dp") for key, g in grads.items() if key not in [piece[:2] for piece in MINE]}
+        mine = group_sum([grads[piece[:2]] for piece in MINE], [piece[1:] for piece in MINE])
+        sums |= {piece[:2]: g for piece, g in zip(MINE, mine)}
+        gradients = [jnp.stack([sums[number, i] for number in range(layers)]).astype(F32) for i in range(3)]
+        new = [adamw(w.astype(F32), m, v, g) for w, m, v, g in zip(weights, m, v, gradients, strict=True)]
         return tuple(one[which] for which in range(3) for one in new)
 
     return jax.shard_map(

time: 514 us -> 422 us (0.82)
  waiting for transfers between devices: 307 us -> 113 us
  Pallas kernels: 0 us -> 98.5 us
  other arithmetic: 67.9 us -> 75.7 us
    psum x1, waiting for transfers between devices: 307 us -> 113 us  [step(): lax.psum(g, 'dp')]
    pallas_call x0 -> x1, Pallas kernels: none -> 98.5 us  [group_sum(): pl.pallas_call(functools.partial(sum_kernel, pieces, [tuple(spec) for spe...]
    convert_element_type x2 -> x3, other arithmetic: 66.4 us -> 74.2 us  [adamw(): return ((w - 0.02 * step).astype(jnp.bfloat16), m, v)]
  transfers between devices with their start and end apart: 1 -> 1, of which waited for: 1 -> 1; matrix products, arithmetic and copies ran while one was open for 0% -> 17% of each run, Pallas kernels for 0% -> 24%
where the time goes in v2:
time: 422 us; the launch traced here: 413 us
  waiting for transfers between devices  113 us (27%)
  matrix products  107 us (25%)
  Pallas kernels  98.5 us (23%)
  other arithmetic  75.7 us (18%)
  between operations  14.9 us (4%)
  local copies, waits for them, and re-layouts  4.74 us (1%)
    psum x1, waiting for transfers between devices, step(): lax.psum(g, 'dp')  113 us
    pallas_call x1, Pallas kernels, group_sum(): pl.pallas_call(functools.partial(sum_kernel, pieces, [tuple(spec) for spe...  98.5 us
    convert_element_type x3, other arithmetic, adamw(): return ((w - 0.02 * step).astype(jnp.bfloat16), m, v)  74.2 us
    dot_general x5, matrix products, layer(): up = jnp.dot(a, w['w_up'], preferred_element_type=jnp.float32)  38.1 us
    dot_general x5, matrix products, layer(): gate = jnp.dot(a, w['w_gate'], preferred_element_type=jnp.float32)  35.6 us
    dot_general x5, matrix products, matmul(): jnp.dot(a, w, preferred_element_type=jnp.float32).astype(jnp.bfloat16)  33 us
  transfers between devices with their start and end apart: 1, of which 1 were waited for; matrix products, arithmetic and copies ran while one was open for 17% of the time, Pallas kernels for 24%

profile of v2, /device:TPU:2, one launch (start us, length us, event | category | flops | bytes accessed | tf_op | source)
XLA Modules:
  0.0 413.5 jit_solution(13269584679920521012)
XLA Ops:
  7.2 0.0 all-reduce.3.cloned.1.call-start
  7.2 1.7 copy.20
  8.9 0.0 copy-start
  9.0 0.0 slice-start
  9.0 0.0 slice-start.4
  9.0 0.4 fusion.36
  9.4 0.0 slice-start.1
  9.4 0.0 copy-start.3
  9.4 0.0 slice-start.5
  9.4 8.6 %convolution_convert_fusion.1 = bf16[1024,2048]{1,0:T(8,128)(2,1)} fusion(bf16[2,2048,768]{2,1,0:T(8,128)(2,1)} %param.15, bf16[1,1024,768]{2,1,0:T(8,128)(2,1)} %param.12), kind=kOutput, calls=%fused_computation.62 | convolution fusion | flops 3223322624 | bytes 8912896 | tf_op jit(solution)/shard_map/transpose(jvp())/dot_general | solution.py:21
  18.0 0.0 slice-done
  18.0 0.0 slice-done.1
  18.0 0.0 copy-done.3
  18.0 0.0 slice-start.6
  18.0 5.7 %fusion.56 = f32[1024,2048]{1,0:T(8,128)} fusion(bf16[2,768,2048]{2,1,0:T(8,128)(2,1)S(1)} %bitcast.77, bf16[1,1024,768]{2,1,0:T(8,128)(2,1)S(1)} %copy-done.3, f32[1024]{0:T(1024)S(1)} %add_rsqrt_fusion), kind=kOutput, calls=%fused_computation.89 | convolution fusion | flops 3223584768 | bytes 13111296 | tf_op jit(solution)/shard_map/dot_general | solution.py:32
  23.7 0.0 slice-done.4
  23.7 0.0 slice-done.5
  23.7 9.3 %multiply_convert_fusion.1 = (bf16[1024,2048]{1,0:T(8,128)(2,1)}, f32[1024,2048]{1,0:T(8,128)}) fusion(f32[1024,2048]{1,0:T(8,128)} %fusion.56, bf16[2,768,2048]{2,1,0:T(8,128)(2,1)S(1)} %bitcast.81, bf16[1,1024,768]{2,1,0:T(8,128)(2,1)S(1)} %copy-done.3, f32[1024]{0:T(1024)S(1)} %add_rsqrt_fusion), kind=kOutput, calls=%fused_computation.44 | convolution fusion | flops 3236167680 | bytes 25694208 | tf_op jit(solution)/shard_map/dot_general | solution.py:33
  33.1 0.0 copy-done
  33.1 0.0 slice-done.6
  33.1 0.0 slice-done.7
  33.1 5.9 %fusion.40 = (f32[1024]{0:T(1024)S(1)}, bf16[1024,768]{0,1:T(8,128)(2,1)S(1)}) fusion(bf16[1024,2048]{1,0:T(8,128)(2,1)} %get-tuple-element.28, bf16[2,2048,768]{2,1,0:T(8,128)(2,1)S(1)} %bitcast.83, bf16[1,1024,768]{1,2,0:T(8,128)(2,1)S(1)} %copy.20), kind=kOutput, calls=%fused_computation.73 | convolution fusion | flops 3225156608 | bytes 10489856 | tf_op jit(solution)/shard_map/dot_general | solution.py:21
  39.0 0.0 copy-start.5
  39.0 5.8 %fusion.48 = f32[1024,2048]{1,0:T(8,128)} fusion(bf16[2,768,2048]{2,1,0:T(8,128)(2,1)S(1)} %bitcast.81, bf16[1024,768]{0,1:T(8,128)(2,1)S(1)} %get-tuple-element.31, f32[1024]{0:T(1024)S(1)} %fusion.96), kind=kOutput, calls=%fused_computation.81 | convolution fusion | flops 3223584768 | bytes 13111296 | tf_op jit(solution)/shard_map/jvp()/dot_general | solution.py:33
  44.8 12.7 %fusion.17 = (bf16[1024,2048]{1,0:T(8,128)(2,1)}, f32[1024,2048]{1,0:T(8,128)}) fusion(f32[1024,2048]{1,0:T(8,128)} %fusion.48, bf16[1024,2048]{1,0:T(8,128)(2,1)} %convolution_convert_fusion.1, bf16[2,768,2048]{2,1,0:T(8,128)(2,1)S(1)} %bitcast.77, bf16[1024,768]{0,1:T(8,128)(2,1)S(1)} %get-tuple-element.31, f32[1024]{0:T(1024)S(1)} %fusion.96), kind=kOutput, calls=%fused_computation.35 | convolution fusion | flops 3248750592 | bytes 29888512 | tf_op jit(solution)/shard_map/jvp()/dot_general | solution.py:32
  57.5 0.0 copy-done.4
  57.5 0.0 copy-done.7
  57.5 0.0 copy-start.11
  57.5 9.9 %fusion.62 = bf16[1,2048,768]{2,1,0:T(8,128)(2,1)} fusion(f32[1024,2048]{1,0:T(8,128)S(1)} %copy-done.7, bf16[1,1024,768]{2,1,0:T(8,128)(2,1)S(1)} %copy-done.4, f32[1024,2048]{1,0:T(8,128)} %get-tuple-element.33), kind=kOutput, calls=%fused_computation.96 | convolution fusion | flops 3235381248 | bytes 21495808 | tf_op jit(solution)/shard_map/transpose(jvp())/dot_general | solution.py:21
  67.4 0.0 copy-done.5
  67.4 0.0 copy-done.11
  67.4 8.7 %fusion.61 = bf16[1,768,2048]{2,1,0:T(8,128)(2,1)} fusion(bf16[1024,2048]{1,0:T(8,128)(2,1)S(1)} %copy-done.11, bf16[1024,768]{0,1:T(8,128)(2,1)S(1)} %get-tuple-element.31, f32[1024]{0:T(1024)S(1)} %fusion.96, f32[1024,2048]{1,0:T(8,128)} %get-tuple-element.33), kind=kOutput, calls=%fused_computation.95 | convolution fusion | flops 3237740544 | bytes 17305600 | tf_op jit(solution)/shard_map/transpose(jvp())/dot_general | solution.py:33
  76.1 0.0 all-reduce.3.cloned.1.call-update
  76.1 2.9 copy.21
  79.0 0.0 slice-start.3
  79.0 0.0 copy-start.6
  79.0 0.0 copy-start.8
  79.1 9.2 %fusion.75 = bf16[1024,768]{0,1:T(8,128)(2,1)S(1)} fusion(bf16[2,768,2048]{2,1,0:T(8,128)(2,1)} %param.14, bf16[1024,2048]{1,0:T(8,128)(2,1)} %convolution_convert_fusion.1, f32[1024,2048]{1,0:T(8,128)} %get-tuple-element.33), kind=kOutput, calls=%fused_computation.105 | convolution fusion | flops 3234594816 | bytes 17301504 | tf_op jit(solution)/shard_map/transpose(jvp())/dot_general | solution.py:33
  88.3 0.0 slice-start.8
  88.3 0.0 slice-done.2
  88.3 0.0 slice-done.3
  88.3 0.0 copy-done.6
  88.3 0.0 copy-start.2
  88.3 0.0 slice-start.9
  88.3 3.8 fusion.42
  92.1 0.0 slice-start.12
  92.1 1.1 fusion.79
  93.3 0.0 copy-start.1
  93.3 0.0 slice-start.13
  93.3 3.7 convolution_convert_fusion
  97.1 0.0 slice-done.12
  97.1 0.0 copy-done.1
  97.1 0.0 slice-done.13
  97.1 5.1 %fusion.35.refs_2_ = bf16[768,2048]{1,0:T(8,128)(2,1)} fusion(bf16[1024,2048]{1,0:T(8,128)(2,1)S(1)} %convolution_convert_fusion, f32[1024,2048]{1,0:T(8,128)S(1)} %bitcast.93, bf16[1,1024,768]{1,2,0:T(8,128)(2,1)S(1)} %copy-done.1, f32[1024]{0:T(1024)S(1)} %add_rsqrt_fusion), kind=kOutput, calls=%fused_computation.66 | convolution fusion | flops 3237740544 | bytes 17305600 | tf_op jit(solution)/shard_map/transpose(jvp())/dot_general | solution.py:33
  102.2 8.6 %fusion.31.refs_3_ = bf16[768,2048]{1,0:T(8,128)(2,1)} fusion(f32[1024,2048]{1,0:T(8,128)S(1)} %bitcast.93, f32[1024,2048]{1,0:T(8,128)} %get-tuple-element.29, bf16[1024,2048]{1,0:T(8,128)(2,1)S(1)} %convolution_convert_fusion, bf16[1,1024,768]{1,2,0:T(8,128)(2,1)S(1)} %copy-done.1, f32[1024]{0:T(1024)S(1)} %add_rsqrt_fusion), kind=kOutput, calls=%fused_computation.64 | convolution fusion | flops 3248226304 | bytes 25694208 | tf_op jit(solution)/shard_map/transpose(jvp())/dot_general | solution.py:32
  110.9 4.9 %convolution_convert_fusion.2.refs_1_ = bf16[2048,768]{1,0:T(8,128)(2,1)} fusion(bf16[1024,2048]{1,0:T(8,128)(2,1)S(1)} %copy-done.10, bf16[1024,768]{0,1:T(8,128)(2,1)S(1)} %fusion.79), kind=kOutput, calls=%fused_computation.67 | convolution fusion | flops 3222798336 | bytes 8912896 | tf_op jit(solution)/shard_map/transpose(jvp())/dot_general | solution.py:21
  115.8 0.0 copy-done.9
  115.8 4.8 %convolution_convert_fusion.3.refs_0_ = bf16[768,2048]{1,0:T(8,128)(2,1)} fusion(bf16[1024,2048]{1,0:T(8,128)(2,1)S(1)} %copy-done.9, bf16[1024,768]{0,1:T(8,128)(2,1)S(1)} %copy-done.6, f32[1024]{0:T(1024)S(1)} %fusion.96), kind=kOutput, calls=%fused_computation.68 | convolution fusion | flops 3223584768 | bytes 8916992 | tf_op jit(solution)/shard_map/transpose(jvp())/dot_general | solution.py:32
  120.6 98.5 %group_sum.1 = (bf16[768,2048]{1,0:T(8,128)(2,1)}, bf16[2048,768]{1,0:T(8,128)(2,1)}, bf16[768,2048]{1,0:T(8,128)(2,1)}, bf16[768,2048]{1,0:T(8,128)(2,1)}) custom-call(bf16[768,2048]{1,0:T(8,128)(2,1)} %convolution_convert_fusion.3.refs_0_, bf16[2048,768]{1,0:T(8,128)(2,1)} %convolution_convert_fusion.2.refs_1_, bf16[768,2048]{1,0:T(8,128)(2,1)} %fusion.35.refs_2_, ...), custom_call_target="tpu_custom_call" | custom-call | flops 300000000 | bytes 60000000 | tf_op jit(solution)/shard_map/group_sum/pallas_call | solution.py:339
  219.1 0.0 slice-start.10
  219.2 25.9 %fusion.2 = (bf16[2,768,2048]{2,1,0:T(8,128)(2,1)}, f32[2,768,2048]{2,1,0:T(8,128)}, f32[2,768,2048]{2,1,0:T(8,128)}) fusion(bf16[2,768,2048]{2,1,0:T(8,128)(2,1)} %param.13, bf16[1,768,2048]{2,1,0:T(8,128)(2,1)} %bitcast.90, bf16[1,768,2048]{2,1,0:T(8,128)(2,1)} %bitcast.91, f32[2,768,2048]{2,1,0:T(8,128)} %param.19, f32[2,768,2048]{2,1,0:T(8,128)} %param.16), kind=kLoop, calls=%fused_computation.14 | loop fusion | flops 59768832 | bytes 69206016 | tf_op jit(solution)/shard_map/convert_element_type | solution.py:355
  245.1 112.8 %all-reduce.3.cloned.1.call-done = (bf16[1,768,2048]{2,1,0:T(8,128)(2,1)}, bf16[1,2048,768]{2,1,0:T(8,128)(2,1)}) async-done(((bf16[1,768,2048]{2,1,0:T(8,128)(2,1)}, bf16[1,2048,768]{2,1,0:T(8,128)(2,1)}), (bf16[1,768,2048]{2,1,0:T(8,128)(2,1)}, bf16[1,2048,768]{2,1,0:T(8,128)(2,1)})) %all-reduce.3.cloned.1.call-update) | async-done | bytes 6291472 | tf_op jit(solution)/shard_map/psum | solution.py:372
  357.9 25.7 %fusion.6 = (bf16[2,768,2048]{2,1,0:T(8,128)(2,1)}, f32[2,768,2048]{2,1,0:T(8,128)}, f32[2,768,2048]{2,1,0:T(8,128)}) fusion(bf16[2,768,2048]{2,1,0:T(8,128)(2,1)} %param.14, bf16[1,768,2048]{2,1,0:T(8,128)(2,1)} %get-tuple-element.17, bf16[1,768,2048]{2,1,0:T(8,128)(2,1)} %bitcast.89, f32[2,768,2048]{2,1,0:T(8,128)} %param.20, f32[2,768,2048]{2,1,0:T(8,128)} %param.17), kind=kLoop, calls=%fused_computation.18 | loop fusion | flops 59768832 | bytes 69206016 | tf_op jit(solution)/shard_map/convert_element_type | solution.py:355
  383.6 22.6 %fusion.10 = (bf16[2,2048,768]{2,1,0:T(8,128)(2,1)}, f32[2,2048,768]{2,1,0:T(8,128)}, f32[2,2048,768]{2,1,0:T(8,128)}) fusion(bf16[2,2048,768]{2,1,0:T(8,128)(2,1)S(1)} %bitcast.87, bf16[1,2048,768]{2,1,0:T(8,128)(2,1)} %get-tuple-element.18, bf16[1,2048,768]{2,1,0:T(8,128)(2,1)} %bitcast.88, f32[2,2048,768]{2,1,0:T(8,128)} %param.21, f32[2,2048,768]{2,1,0:T(8,128)} %param.18), kind=kLoop, calls=%fused_computation.22 | loop fusion | flops 59768832 | bytes 69206016 | tf_op jit(solution)/shard_map/convert_element_type | solution.py:355
  (24 shorter events, 0.1 us)
Async XLA Ops:
  7.2 350.7 %all-reduce.3.cloned.1.call-start = ((), (), s32[]{:S(2)}) async-start(), calls=%async_computation | async-start | bytes 12582912 | tf_op jit(solution)/shard_map/psum | solution.py:372
  8.9 24.1 %copy-start = (bf16[1,1024,768]{1,2,0:T(8,128)(2,1)}, bf16[1,1024,768]{1,2,0:T(8,128)(2,1)S(1)}, u32[]{:S(2)}) copy-start(bf16[1,1024,768]{1,2,0:T(8,128)(2,1)S(1)} %copy.20) | copy-start | bytes 4718596
  9.0 9.0 %slice-start = ((s8[6291456]{0:T(1024)(128)(4,1)}), s8[4194304]{0:T(1024)(128)(4,1)S(1)}, s32[]{:S(2)}) async-start(s8[6291456]{0:T(1024)(128)(4,1)} %bitcast.76), calls=%async_computation.1 | async-start | bytes 8388608
  9.0 14.8 %slice-start.4 = ((s8[6291456]{0:T(1024)(128)(4,1)}), s8[4194304]{0:T(1024)(128)(4,1)S(1)}, s32[]{:S(2)}) async-start(s8[6291456]{0:T(1024)(128)(4,1)} %bitcast.80), calls=%async_computation.5 | async-start | bytes 8388608
  9.4 8.6 %slice-start.1 = ((s8[6291456]{0:T(1024)(128)(4,1)}), s8[2097152]{0:T(1024)(128)(4,1)S(1)}, s32[]{:S(2)}) async-start(s8[6291456]{0:T(1024)(128)(4,1)} %bitcast.76), calls=%async_computation.2 | async-start | bytes 4194304
  9.4 8.6 %copy-start.3 = (bf16[1,1024,768]{2,1,0:T(8,128)(2,1)S(1)}, bf16[1,1024,768]{2,1,0:T(8,128)(2,1)}, u32[]{:S(2)}) copy-start(bf16[1,1024,768]{2,1,0:T(8,128)(2,1)} %param.11) | copy-start | bytes 4718596
  9.4 14.4 %slice-start.5 = ((s8[6291456]{0:T(1024)(128)(4,1)}), s8[2097152]{0:T(1024)(128)(4,1)S(1)}, s32[]{:S(2)}) async-start(s8[6291456]{0:T(1024)(128)(4,1)} %bitcast.80), calls=%async_computation.6 | async-start | bytes 4194304
  18.0 15.1 %slice-start.6 = ((s8[6291456]{0:T(1024)(128)(4,1)}), s8[4194304]{0:T(1024)(128)(4,1)S(1)}, s32[]{:S(2)}) async-start(s8[6291456]{0:T(1024)(128)(4,1)} %bitcast.82), calls=%async_computation.7 | async-start | bytes 8388608
  23.7 9.3 %slice-start.7 = ((s8[6291456]{0:T(1024)(128)(4,1)}), s8[2097152]{0:T(1024)(128)(4,1)S(1)}, s32[]{:S(2)}) async-start(s8[6291456]{0:T(1024)(128)(4,1)} %bitcast.82), calls=%async_computation.8 | async-start | bytes 4194304
  39.0 28.3 %copy-start.5 = (bf16[1024,768]{0,1:T(8,128)(2,1)}, bf16[1024,768]{0,1:T(8,128)(2,1)S(1)}, u32[]{:S(2)}) copy-start(bf16[1024,768]{0,1:T(8,128)(2,1)S(1)} %get-tuple-element.31) | copy-start | bytes 4718596
  44.8 12.7 %copy-start.4 = (bf16[1,1024,768]{2,1,0:T(8,128)(2,1)S(1)}, bf16[1,1024,768]{2,1,0:T(8,128)(2,1)}, u32[]{:S(2)}) copy-start(bf16[1,1024,768]{2,1,0:T(8,128)(2,1)} %param.12) | copy-start | bytes 4718596
  44.8 12.7 %copy-start.7 = (f32[1024,2048]{1,0:T(8,128)S(1)}, f32[1024,2048]{1,0:T(8,128)}, u32[]{:S(2)}) copy-start(f32[1024,2048]{1,0:T(8,128)} %fusion.48) | copy-start | bytes 25165828
  57.5 9.9 %copy-start.11 = (bf16[1024,2048]{1,0:T(8,128)(2,1)S(1)}, bf16[1024,2048]{1,0:T(8,128)(2,1)}, u32[]{:S(2)}) copy-start(bf16[1024,2048]{1,0:T(8,128)(2,1)} %convolution_convert_fusion.1) | copy-start | bytes 12582916
  76.1 12.2 %slice-start.2 = ((s8[6291456]{0:T(1024)(128)(4,1)}), s8[2097152]{0:T(1024)(128)(4,1)S(1)}, s32[]{:S(2)}) async-start(s8[6291456]{0:T(1024)(128)(4,1)} %bitcast.78), calls=%async_computation.3 | async-start | bytes 4194304
  79.0 9.3 %slice-start.3 = ((s8[6291456]{0:T(1024)(128)(4,1)}), s8[4194304]{0:T(1024)(128)(4,1)S(1)}, s32[]{:S(2)}) async-start(s8[6291456]{0:T(1024)(128)(4,1)} %bitcast.78), calls=%async_computation.4 | async-start | bytes 8388608
  79.0 9.3 %copy-start.6 = (bf16[1024,768]{0,1:T(8,128)(2,1)S(1)}, bf16[1024,768]{0,1:T(8,128)(2,1)}, u32[]{:S(2)}) copy-start(bf16[1024,768]{0,1:T(8,128)(2,1)} %copy-done.5) | copy-start | bytes 4718596
  79.0 9.3 %copy-start.8 = (bf16[1024,2048]{1,0:T(8,128)(2,1)S(1)}, bf16[1024,2048]{1,0:T(8,128)(2,1)}, u32[]{:S(2)}) copy-start(bf16[1024,2048]{1,0:T(8,128)(2,1)} %get-tuple-element.32) | copy-start | bytes 12582916
  88.3 5.0 %slice-start.8 = ((s8[6291456]{0:T(1024)(128)(4,1)}), s8[4194304]{0:T(1024)(128)(4,1)S(1)}, s32[]{:S(2)}) async-start(s8[6291456]{0:T(1024)(128)(4,1)} %bitcast.84), calls=%async_computation.9 | async-start | bytes 8388608
  88.3 3.8 copy-start.2
  88.3 5.0 %slice-start.9 = ((s8[6291456]{0:T(1024)(128)(4,1)}), s8[2097152]{0:T(1024)(128)(4,1)S(1)}, s32[]{:S(2)}) async-start(s8[6291456]{0:T(1024)(128)(4,1)} %bitcast.84), calls=%async_computation.10 | async-start | bytes 4194304
  92.1 5.0 %slice-start.12 = ((s8[8388608]{0:T(1024)(128)(4,1)}), s8[4194304]{0:T(1024)(128)(4,1)S(1)}, s32[]{:S(2)}) async-start(s8[8388608]{0:T(1024)(128)(4,1)} %bitcast.92), calls=%async_computation.13 | async-start | bytes 8388608
  93.3 3.8 copy-start.1
  93.3 3.8 slice-start.13
  102.2 8.6 %copy-start.10 = (bf16[1024,2048]{1,0:T(8,128)(2,1)S(1)}, bf16[1024,2048]{1,0:T(8,128)(2,1)}, u32[]{:S(2)}) copy-start(bf16[1024,2048]{1,0:T(8,128)(2,1)} %get-tuple-element.28) | copy-start | bytes 12582916
  110.9 4.9 %copy-start.9 = (bf16[1024,2048]{1,0:T(8,128)(2,1)S(1)}, bf16[1024,2048]{1,0:T(8,128)(2,1)}, u32[]{:S(2)}) copy-start(bf16[1024,2048]{1,0:T(8,128)(2,1)} %get-tuple-element.32) | copy-start | bytes 12582916
  219.1 164.4 %slice-start.10 = ((s8[6291456]{0:T(1024)(128)(4,1)}), s8[2097152]{0:T(1024)(128)(4,1)S(1)}, s32[]{:S(2)}) async-start(s8[6291456]{0:T(1024)(128)(4,1)} %bitcast.86), calls=%async_computation.11 | async-start | bytes 4194304
  357.9 25.7 %slice-start.11 = ((s8[6291456]{0:T(1024)(128)(4,1)}), s8[4194304]{0:T(1024)(128)(4,1)S(1)}, s32[]{:S(2)}) async-start(s8[6291456]{0:T(1024)(128)(4,1)} %bitcast.86), calls=%async_computation.12 | async-start | bytes 8388608
Sparse Core Ops, SparseCore 0:
  76.3 281.5 all-reduce.2
